TPU v7x, 32 devices: a 4x4x1 block of a 4x4x8 slice. The times are simulated.
32 devices in a mesh: sys: 1 (over z), row: 32 (over y, x, core).
Axes of the slice: x: 4, y: 4, z: 1, core: 2. Of those that a mesh axis runs over, the one named last changes fastest.
The devices are a block of a 4x4x8 slice.
Arguments:
- positions: bfloat16 [32768, 128], P(('sys', 'row'))
- charges: float32 [32768], P(('sys', 'row'))
- counts: int32 [32], P(('sys', 'row'))
Outputs:
- output 1: float32 [32768, 128], P(('sys', 'row'))
- output 2: float32 [1], P('sys')
All inputs are finite; a program needn't handle non-finite values.
Results may differ from a plain program's by a relative error of at most 0.001.
Values are sent between devices in bfloat16 or wider.
A program may use at most 768 MiB of HBM per device.

v0:
```python
import jax
import jax.numpy as jnp
from jax import lax
from jax.sharding import PartitionSpec as P


def sq_norm(block_pos):
    pos_f32 = block_pos.astype(jnp.float32)
    return jnp.sum(pos_f32 * pos_f32, axis=1)


def pair_weight(row_pos, row_q, col_pos, col_q, neg_scale):
    gram_mat = jnp.einsum('id,jd->ij', row_pos, col_pos, preferred_element_type=jnp.float32)
    dist_sq = jnp.maximum(sq_norm(row_pos)[:, None] + sq_norm(col_pos)[None, :] - 2.0 * gram_mat, 0.0)
    return row_q[:, None] * col_q[None, :] * jnp.exp(dist_sq * neg_scale)


def row_force(weight, w_low, row_pos, col_pos, inv_len2):
    pulled = jnp.dot(w_low, col_pos, preferred_element_type=jnp.float32)
    return (jnp.sum(weight, axis=1)[:, None] * row_pos.astype(jnp.float32) - pulled) * inv_len2


def col_force(weight, w_low, row_pos, col_pos, inv_len2):
    pushed = jnp.einsum('ij,id->jd', w_low, row_pos, preferred_element_type=jnp.float32)
    return (jnp.sum(weight, axis=0)[:, None] * col_pos.astype(jnp.float32) - pushed) * inv_len2


def solution(mesh):
    num_blocks = mesh.shape['row']
    half_way = num_blocks // 2
    next_perm = [(src, (src + 1) % num_blocks) for src in range(num_blocks)]
    home_perm = [(src, (src - half_way) % num_blocks) for src in range(num_blocks)]

    def per_device(positions, charges, counts):
        block_rows, width = positions.shape
        half_rows = block_rows // 2
        neg_scale = -0.5 / width
        inv_len2 = 1.0 / width
        live_q = jnp.where(jnp.arange(block_rows) < counts[0], charges, 0.0)
        diag_mask = jnp.arange(block_rows)[:, None] == jnp.arange(block_rows)[None, :]
        own_w = jnp.where(diag_mask, 0.0, pair_weight(positions, live_q, positions, live_q, neg_scale))
        own_force = row_force(own_w, own_w.astype(jnp.bfloat16), positions, positions, inv_len2)
        energy = 0.5 * jnp.sum(own_w)
        vis_pos = lax.ppermute(positions, 'row', next_perm)
        vis_q = lax.ppermute(live_q, 'row', next_perm)
        vis_react = jnp.zeros((block_rows, width), jnp.float32)

        def full_step(step_idx, loop_state):
            vis_pos, vis_q, vis_react, own_force, energy = loop_state
            weight = pair_weight(positions, live_q, vis_pos, vis_q, neg_scale)
            w_low = weight.astype(jnp.bfloat16)
            own_force = own_force + row_force(weight, w_low, positions, vis_pos, inv_len2)
            vis_react = vis_react + col_force(weight, w_low, positions, vis_pos, inv_len2)
            energy = energy + jnp.sum(weight)
            vis_pos = lax.ppermute(vis_pos, 'row', next_perm)
            vis_q = lax.ppermute(vis_q, 'row', next_perm)
            vis_react = lax.ppermute(vis_react, 'row', next_perm)
            return vis_pos, vis_q, vis_react, own_force, energy

        loop_state = lax.fori_loop(0, half_way - 1, full_step, (vis_pos, vis_q, vis_react, own_force, energy))
        vis_pos, vis_q, vis_react, own_force, energy = loop_state
        is_lower = lax.axis_index('row') < half_way
        a_pos = jnp.where(is_lower, positions[:half_rows], vis_pos[half_rows:])
        a_q = jnp.where(is_lower, live_q[:half_rows], vis_q[half_rows:])
        b_pos = jnp.where(is_lower, vis_pos, positions)
        b_q = jnp.where(is_lower, vis_q, live_q)
        weight = pair_weight(a_pos, a_q, b_pos, b_q, neg_scale)
        w_low = weight.astype(jnp.bfloat16)
        a_force = row_force(weight, w_low, a_pos, b_pos, inv_len2)
        b_force = col_force(weight, w_low, a_pos, b_pos, inv_len2)
        zero_half = jnp.zeros((half_rows, width), jnp.float32)
        own_force = own_force + jnp.where(is_lower, jnp.concatenate([a_force, zero_half], axis=0), b_force)
        vis_react = vis_react + jnp.where(is_lower, b_force, jnp.concatenate([zero_half, a_force], axis=0))
        energy = energy + jnp.sum(weight)
        own_force = own_force + lax.ppermute(vis_react, 'row', home_perm)
        energy = lax.psum(energy, 'row')
        return own_force, energy.reshape(1)

    row_spec = P(('sys', 'row'), None)
    vec_spec = P(('sys', 'row'))
    return jax.shard_map(per_device, mesh=mesh, in_specs=(row_spec, vec_spec, vec_spec), out_specs=(row_spec, P('sys')), check_vma=False)
```

profile of v0, /device:TPU:97, one launch (start us, length us, event | category | flops | bytes accessed | tf_op | source)
XLA Modules:
  0.0 358.6 jit_solution(16321074094450215259)
XLA Ops:
  2.0 2.7 collective-permute-start.4
  4.7 1.2 fusion.18
  5.8 3.9 %fusion.25 = (f32[]{:T(128)}, f32[1024]{0:T(1024)S(1)}, bf16[1024,1024]{0,1:T(8,128)(2,1)S(1)}) fusion(bf16[1024,128]{1,0:T(8,128)(2,1)} %param.5, f32[1024]{0:T(1024)S(1)} %fusion.18, f32[1024]{0:T(1024)S(1)} %fusion.23), kind=kOutput, calls=%fused_computation.46 | convolution fusion | flops 281017344 | bytes 2371588 | tf_op jit(solution)/shard_map/id,jd->ij/dot_general | solution.py:13
  11.3 280.9 %while.18 = (s32[]{:T(128)}, bf16[1024,128]{1,0:T(8,128)(2,1)S(1)}, f32[1024]{0:T(1024)S(1)}, f32[1024,128]{1,0:T(8,128)S(1)}, f32[1024,128]{1,0:T(8,128)S(1)}, ...) while((s32[]{:T(128)}, bf16[1024,128]{1,0:T(8,128)(2,1)S(1)}, ...), condition=%wide.region_9.10_spmd, body=%wide.region_3.9_spmd.sunk | while | flops 818933760 | bytes 14221541 | solution.py:60
  11.7 3.4 fusion.60
  15.9 1.8 collective-permute-start.2
  17.8 1.3 collective-permute-start.1
  20.6 6.1 %collective-permute-done.1 = f32[1024]{0:T(1024)S(1)} collective-permute-done((f32[1024]{0:T(1024)S(1)}, f32[1024]{0:T(1024)S(1)}, u32[]{:S(2)}, u32[]{:S(2)}) %collective-permute-start.1) | collective-permute-done | bytes 4128 | tf_op jit(solution)/shard_map/while/body/eval_jaxpr/ppermute | solution.py:56
  27.0 3.4 fusion.60
  30.4 0.8 fusion.61
  31.1 2.6 collective-permute-start.2
  33.9 1.3 collective-permute-start.1
  36.6 6.1 %collective-permute-done.1 = f32[1024]{0:T(1024)S(1)} collective-permute-done((f32[1024]{0:T(1024)S(1)}, f32[1024]{0:T(1024)S(1)}, u32[]{:S(2)}, u32[]{:S(2)}) %collective-permute-start.1) | collective-permute-done | bytes 4128 | tf_op jit(solution)/shard_map/while/body/eval_jaxpr/ppermute | solution.py:56
  43.1 3.4 fusion.60
  46.5 0.8 fusion.61
  47.2 2.6 collective-permute-start.2
  49.9 1.3 collective-permute-start.1
  52.7 6.8 %collective-permute-done.1 = f32[1024]{0:T(1024)S(1)} collective-permute-done((f32[1024]{0:T(1024)S(1)}, f32[1024]{0:T(1024)S(1)}, u32[]{:S(2)}, u32[]{:S(2)}) %collective-permute-start.1) | collective-permute-done | bytes 4128 | tf_op jit(solution)/shard_map/while/body/eval_jaxpr/ppermute | solution.py:56
  59.9 3.4 fusion.60
  63.3 0.8 fusion.61
  64.0 1.9 collective-permute-start.2
  66.0 1.3 collective-permute-start.1
  68.8 10.1 %collective-permute-done.1 = f32[1024]{0:T(1024)S(1)} collective-permute-done((f32[1024]{0:T(1024)S(1)}, f32[1024]{0:T(1024)S(1)}, u32[]{:S(2)}, u32[]{:S(2)}) %collective-permute-start.1) | collective-permute-done | bytes 4128 | tf_op jit(solution)/shard_map/while/body/eval_jaxpr/ppermute | solution.py:56
  79.3 3.4 fusion.60
  85.2 13.1 %collective-permute-done.1 = f32[1024]{0:T(1024)S(1)} collective-permute-done((f32[1024]{0:T(1024)S(1)}, f32[1024]{0:T(1024)S(1)}, u32[]{:S(2)}, u32[]{:S(2)}) %collective-permute-start.1) | collective-permute-done | bytes 4128 | tf_op jit(solution)/shard_map/while/body/eval_jaxpr/ppermute | solution.py:56
  98.7 3.4 fusion.60
  104.6 13.1 %collective-permute-done.1 = f32[1024]{0:T(1024)S(1)} collective-permute-done((f32[1024]{0:T(1024)S(1)}, f32[1024]{0:T(1024)S(1)}, u32[]{:S(2)}, u32[]{:S(2)}) %collective-permute-start.1) | collective-permute-done | bytes 4128 | tf_op jit(solution)/shard_map/while/body/eval_jaxpr/ppermute | solution.py:56
  118.1 3.4 fusion.60
  124.0 13.1 %collective-permute-done.1 = f32[1024]{0:T(1024)S(1)} collective-permute-done((f32[1024]{0:T(1024)S(1)}, f32[1024]{0:T(1024)S(1)}, u32[]{:S(2)}, u32[]{:S(2)}) %collective-permute-start.1) | collective-permute-done | bytes 4128 | tf_op jit(solution)/shard_map/while/body/eval_jaxpr/ppermute | solution.py:56
  137.5 3.4 fusion.60
  143.4 13.1 %collective-permute-done.1 = f32[1024]{0:T(1024)S(1)} collective-permute-done((f32[1024]{0:T(1024)S(1)}, f32[1024]{0:T(1024)S(1)}, u32[]{:S(2)}, u32[]{:S(2)}) %collective-permute-start.1) | collective-permute-done | bytes 4128 | tf_op jit(solution)/shard_map/while/body/eval_jaxpr/ppermute | solution.py:56
  156.9 3.4 fusion.60
  162.8 13.1 %collective-permute-done.1 = f32[1024]{0:T(1024)S(1)} collective-permute-done((f32[1024]{0:T(1024)S(1)}, f32[1024]{0:T(1024)S(1)}, u32[]{:S(2)}, u32[]{:S(2)}) %collective-permute-start.1) | collective-permute-done | bytes 4128 | tf_op jit(solution)/shard_map/while/body/eval_jaxpr/ppermute | solution.py:56
  176.3 3.4 fusion.60
  182.2 13.1 %collective-permute-done.1 = f32[1024]{0:T(1024)S(1)} collective-permute-done((f32[1024]{0:T(1024)S(1)}, f32[1024]{0:T(1024)S(1)}, u32[]{:S(2)}, u32[]{:S(2)}) %collective-permute-start.1) | collective-permute-done | bytes 4128 | tf_op jit(solution)/shard_map/while/body/eval_jaxpr/ppermute | solution.py:56
  195.7 3.4 fusion.60
  201.6 13.1 %collective-permute-done.1 = f32[1024]{0:T(1024)S(1)} collective-permute-done((f32[1024]{0:T(1024)S(1)}, f32[1024]{0:T(1024)S(1)}, u32[]{:S(2)}, u32[]{:S(2)}) %collective-permute-start.1) | collective-permute-done | bytes 4128 | tf_op jit(solution)/shard_map/while/body/eval_jaxpr/ppermute | solution.py:56
  215.1 3.4 fusion.60
  221.0 13.1 %collective-permute-done.1 = f32[1024]{0:T(1024)S(1)} collective-permute-done((f32[1024]{0:T(1024)S(1)}, f32[1024]{0:T(1024)S(1)}, u32[]{:S(2)}, u32[]{:S(2)}) %collective-permute-start.1) | collective-permute-done | bytes 4128 | tf_op jit(solution)/shard_map/while/body/eval_jaxpr/ppermute | solution.py:56
  234.5 3.4 fusion.60
  240.4 13.1 %collective-permute-done.1 = f32[1024]{0:T(1024)S(1)} collective-permute-done((f32[1024]{0:T(1024)S(1)}, f32[1024]{0:T(1024)S(1)}, u32[]{:S(2)}, u32[]{:S(2)}) %collective-permute-start.1) | collective-permute-done | bytes 4128 | tf_op jit(solution)/shard_map/while/body/eval_jaxpr/ppermute | solution.py:56
  253.8 3.4 fusion.60
  259.8 13.1 %collective-permute-done.1 = f32[1024]{0:T(1024)S(1)} collective-permute-done((f32[1024]{0:T(1024)S(1)}, f32[1024]{0:T(1024)S(1)}, u32[]{:S(2)}, u32[]{:S(2)}) %collective-permute-start.1) | collective-permute-done | bytes 4128 | tf_op jit(solution)/shard_map/while/body/eval_jaxpr/ppermute | solution.py:56
  273.2 3.4 fusion.60
  279.2 13.1 %collective-permute-done.1 = f32[1024]{0:T(1024)S(1)} collective-permute-done((f32[1024]{0:T(1024)S(1)}, f32[1024]{0:T(1024)S(1)}, u32[]{:S(2)}, u32[]{:S(2)}) %collective-permute-start.1) | collective-permute-done | bytes 4128 | tf_op jit(solution)/shard_map/while/body/eval_jaxpr/ppermute | solution.py:56
  292.6 1.9 fusion.26
  296.3 61.4 %psum.7 = f32[1]{0:T(128)} all-reduce(f32[1]{0:T(128)} %bitcast.1), channel_id=1, replica_groups=mesh['sys'=1,'row'=32] {'row'}, use_global_device_ids=true, to_apply=%region_15.16 | all-reduce | flops 1 | bytes 8 | tf_op jit(solution)/shard_map/psum | solution.py:76
  357.7 0.9 add_add_fusion
  (158 shorter events, 32.9 us)
Async XLA Ops:
  2.0 9.3 %collective-permute-start.4 = (f32[1024]{0:T(1024)S(1)}, f32[1024]{0:T(1024)S(1)}, u32[]{:S(2)}, u32[]{:S(2)}) collective-permute-start(f32[1024]{0:T(1024)S(1)} %fusion.23), channel_id=1, source_target_pairs={{0,1},{1,2},{2,3},{3,4},{4,5},{5,6},{6,7},{7,8},{8,9},{9,10},{10,1... | collective-permute-start | bytes 12296 | tf_op jit(solution)/shard_map/ppermute | solution.py:45
  4.6 6.6 %collective-permute-start.3 = (bf16[1024,128]{1,0:T(8,128)(2,1)}, bf16[1024,128]{1,0:T(8,128)(2,1)S(1)}, u32[]{:S(2)}, u32[]{:S(2)}) collective-permute-start(bf16[1024,128]{1,0:T(8,128)(2,1)} %param.5), channel_id=1, source_target_pairs={{0,1},{1,2},{2,3},{3,4},{4,5},{5,6},{6,7},{7,8},{8,9},{9,10},{10,1... | collective-permute-start | bytes 786440 | tf_op jit(solution)/shard_map/ppermute | solution.py:44
  15.9 10.8 %collective-permute-start.2 = (f32[1024,128]{1,0:T(8,128)S(1)}, f32[1024,128]{1,0:T(8,128)S(1)}, u32[]{:S(2)}, u32[]{:S(2)}) collective-permute-start(f32[1024,128]{1,0:T(8,128)S(1)} %fusion.61), channel_id=1, source_target_pairs={{0,1},{1,2},{2,3},{3,4},{4,5},{5,6},{6,7},{7,8},{8,9},{9,10},{10,1... | collective-permute-start | bytes 1572872 | tf_op jit(solution)/shard_map/while/body/eval_jaxpr/ppermute | solution.py:57
  17.7 9.0 %collective-permute-start = (bf16[1024,128]{1,0:T(8,128)(2,1)S(1)}, bf16[1024,128]{1,0:T(8,128)(2,1)S(1)}, u32[]{:S(2)}, u32[]{:S(2)}) collective-permute-start(bf16[1024,128]{1,0:T(8,128)(2,1)S(1)} %copy.12), channel_id=1, source_target_pairs={{0,1},{1,2},{2,3},{3,4},{4,5},{5,6},{6,7},{7,8},{8,9},{9,10},{10,1... | collective-permute-start | bytes 786440 | tf_op jit(solution)/shard_map/while/body/eval_jaxpr/ppermute | solution.py:55
  17.8 8.8 %collective-permute-start.1 = (f32[1024]{0:T(1024)S(1)}, f32[1024]{0:T(1024)S(1)}, u32[]{:S(2)}, u32[]{:S(2)}) collective-permute-start(f32[1024]{0:T(1024)S(1)} %copy.13), channel_id=1, source_target_pairs={{0,1},{1,2},{2,3},{3,4},{4,5},{5,6},{6,7},{7,8},{8,9},{9,10},{10,1... | collective-permute-start | bytes 12296 | tf_op jit(solution)/shard_map/while/body/eval_jaxpr/ppermute | solution.py:56
  31.1 11.6 %collective-permute-start.2 = (f32[1024,128]{1,0:T(8,128)S(1)}, f32[1024,128]{1,0:T(8,128)S(1)}, u32[]{:S(2)}, u32[]{:S(2)}) collective-permute-start(f32[1024,128]{1,0:T(8,128)S(1)} %fusion.61), channel_id=1, source_target_pairs={{0,1},{1,2},{2,3},{3,4},{4,5},{5,6},{6,7},{7,8},{8,9},{9,10},{10,1... | collective-permute-start | bytes 1572872 | tf_op jit(solution)/shard_map/while/body/eval_jaxpr/ppermute | solution.py:57
  33.8 9.0 %collective-permute-start = (bf16[1024,128]{1,0:T(8,128)(2,1)S(1)}, bf16[1024,128]{1,0:T(8,128)(2,1)S(1)}, u32[]{:S(2)}, u32[]{:S(2)}) collective-permute-start(bf16[1024,128]{1,0:T(8,128)(2,1)S(1)} %copy.12), channel_id=1, source_target_pairs={{0,1},{1,2},{2,3},{3,4},{4,5},{5,6},{6,7},{7,8},{8,9},{9,10},{10,1... | collective-permute-start | bytes 786440 | tf_op jit(solution)/shard_map/while/body/eval_jaxpr/ppermute | solution.py:55
  33.9 8.8 %collective-permute-start.1 = (f32[1024]{0:T(1024)S(1)}, f32[1024]{0:T(1024)S(1)}, u32[]{:S(2)}, u32[]{:S(2)}) collective-permute-start(f32[1024]{0:T(1024)S(1)} %copy.13), channel_id=1, source_target_pairs={{0,1},{1,2},{2,3},{3,4},{4,5},{5,6},{6,7},{7,8},{8,9},{9,10},{10,1... | collective-permute-start | bytes 12296 | tf_op jit(solution)/shard_map/while/body/eval_jaxpr/ppermute | solution.py:56
  47.2 12.3 %collective-permute-start.2 = (f32[1024,128]{1,0:T(8,128)S(1)}, f32[1024,128]{1,0:T(8,128)S(1)}, u32[]{:S(2)}, u32[]{:S(2)}) collective-permute-start(f32[1024,128]{1,0:T(8,128)S(1)} %fusion.61), channel_id=1, source_target_pairs={{0,1},{1,2},{2,3},{3,4},{4,5},{5,6},{6,7},{7,8},{8,9},{9,10},{10,1... | collective-permute-start | bytes 1572872 | tf_op jit(solution)/shard_map/while/body/eval_jaxpr/ppermute | solution.py:57
  49.8 9.7 %collective-permute-start = (bf16[1024,128]{1,0:T(8,128)(2,1)S(1)}, bf16[1024,128]{1,0:T(8,128)(2,1)S(1)}, u32[]{:S(2)}, u32[]{:S(2)}) collective-permute-start(bf16[1024,128]{1,0:T(8,128)(2,1)S(1)} %copy.12), channel_id=1, source_target_pairs={{0,1},{1,2},{2,3},{3,4},{4,5},{5,6},{6,7},{7,8},{8,9},{9,10},{10,1... | collective-permute-start | bytes 786440 | tf_op jit(solution)/shard_map/while/body/eval_jaxpr/ppermute | solution.py:55
  49.9 9.6 %collective-permute-start.1 = (f32[1024]{0:T(1024)S(1)}, f32[1024]{0:T(1024)S(1)}, u32[]{:S(2)}, u32[]{:S(2)}) collective-permute-start(f32[1024]{0:T(1024)S(1)} %copy.13), channel_id=1, source_target_pairs={{0,1},{1,2},{2,3},{3,4},{4,5},{5,6},{6,7},{7,8},{8,9},{9,10},{10,1... | collective-permute-start | bytes 12296 | tf_op jit(solution)/shard_map/while/body/eval_jaxpr/ppermute | solution.py:56
  64.0 14.9 %collective-permute-start.2 = (f32[1024,128]{1,0:T(8,128)S(1)}, f32[1024,128]{1,0:T(8,128)S(1)}, u32[]{:S(2)}, u32[]{:S(2)}) collective-permute-start(f32[1024,128]{1,0:T(8,128)S(1)} %fusion.61), channel_id=1, source_target_pairs={{0,1},{1,2},{2,3},{3,4},{4,5},{5,6},{6,7},{7,8},{8,9},{9,10},{10,1... | collective-permute-start | bytes 1572872 | tf_op jit(solution)/shard_map/while/body/eval_jaxpr/ppermute | solution.py:57
  65.9 13.0 %collective-permute-start = (bf16[1024,128]{1,0:T(8,128)(2,1)S(1)}, bf16[1024,128]{1,0:T(8,128)(2,1)S(1)}, u32[]{:S(2)}, u32[]{:S(2)}) collective-permute-start(bf16[1024,128]{1,0:T(8,128)(2,1)S(1)} %copy.12), channel_id=1, source_target_pairs={{0,1},{1,2},{2,3},{3,4},{4,5},{5,6},{6,7},{7,8},{8,9},{9,10},{10,1... | collective-permute-start | bytes 786440 | tf_op jit(solution)/shard_map/while/body/eval_jaxpr/ppermute | solution.py:55
  66.0 12.9 %collective-permute-start.1 = (f32[1024]{0:T(1024)S(1)}, f32[1024]{0:T(1024)S(1)}, u32[]{:S(2)}, u32[]{:S(2)}) collective-permute-start(f32[1024]{0:T(1024)S(1)} %copy.13), channel_id=1, source_target_pairs={{0,1},{1,2},{2,3},{3,4},{4,5},{5,6},{6,7},{7,8},{8,9},{9,10},{10,1... | collective-permute-start | bytes 12296 | tf_op jit(solution)/shard_map/while/body/eval_jaxpr/ppermute | solution.py:56
  83.4 14.9 %collective-permute-start.2 = (f32[1024,128]{1,0:T(8,128)S(1)}, f32[1024,128]{1,0:T(8,128)S(1)}, u32[]{:S(2)}, u32[]{:S(2)}) collective-permute-start(f32[1024,128]{1,0:T(8,128)S(1)} %fusion.61), channel_id=1, source_target_pairs={{0,1},{1,2},{2,3},{3,4},{4,5},{5,6},{6,7},{7,8},{8,9},{9,10},{10,1... | collective-permute-start | bytes 1572872 | tf_op jit(solution)/shard_map/while/body/eval_jaxpr/ppermute | solution.py:57
  83.5 14.8 %collective-permute-start = (bf16[1024,128]{1,0:T(8,128)(2,1)S(1)}, bf16[1024,128]{1,0:T(8,128)(2,1)S(1)}, u32[]{:S(2)}, u32[]{:S(2)}) collective-permute-start(bf16[1024,128]{1,0:T(8,128)(2,1)S(1)} %copy.12), channel_id=1, source_target_pairs={{0,1},{1,2},{2,3},{3,4},{4,5},{5,6},{6,7},{7,8},{8,9},{9,10},{10,1... | collective-permute-start | bytes 786440 | tf_op jit(solution)/shard_map/while/body/eval_jaxpr/ppermute | solution.py:55
  83.7 14.6 %collective-permute-start.1 = (f32[1024]{0:T(1024)S(1)}, f32[1024]{0:T(1024)S(1)}, u32[]{:S(2)}, u32[]{:S(2)}) collective-permute-start(f32[1024]{0:T(1024)S(1)} %copy.13), channel_id=1, source_target_pairs={{0,1},{1,2},{2,3},{3,4},{4,5},{5,6},{6,7},{7,8},{8,9},{9,10},{10,1... | collective-permute-start | bytes 12296 | tf_op jit(solution)/shard_map/while/body/eval_jaxpr/ppermute | solution.py:56
  102.8 14.9 %collective-permute-start.2 = (f32[1024,128]{1,0:T(8,128)S(1)}, f32[1024,128]{1,0:T(8,128)S(1)}, u32[]{:S(2)}, u32[]{:S(2)}) collective-permute-start(f32[1024,128]{1,0:T(8,128)S(1)} %fusion.61), channel_id=1, source_target_pairs={{0,1},{1,2},{2,3},{3,4},{4,5},{5,6},{6,7},{7,8},{8,9},{9,10},{10,1... | collective-permute-start | bytes 1572872 | tf_op jit(solution)/shard_map/while/body/eval_jaxpr/ppermute | solution.py:57
  102.9 14.8 %collective-permute-start = (bf16[1024,128]{1,0:T(8,128)(2,1)S(1)}, bf16[1024,128]{1,0:T(8,128)(2,1)S(1)}, u32[]{:S(2)}, u32[]{:S(2)}) collective-permute-start(bf16[1024,128]{1,0:T(8,128)(2,1)S(1)} %copy.12), channel_id=1, source_target_pairs={{0,1},{1,2},{2,3},{3,4},{4,5},{5,6},{6,7},{7,8},{8,9},{9,10},{10,1... | collective-permute-start | bytes 786440 | tf_op jit(solution)/shard_map/while/body/eval_jaxpr/ppermute | solution.py:55
  103.1 14.6 %collective-permute-start.1 = (f32[1024]{0:T(1024)S(1)}, f32[1024]{0:T(1024)S(1)}, u32[]{:S(2)}, u32[]{:S(2)}) collective-permute-start(f32[1024]{0:T(1024)S(1)} %copy.13), channel_id=1, source_target_pairs={{0,1},{1,2},{2,3},{3,4},{4,5},{5,6},{6,7},{7,8},{8,9},{9,10},{10,1... | collective-permute-start | bytes 12296 | tf_op jit(solution)/shard_map/while/body/eval_jaxpr/ppermute | solution.py:56
  122.2 14.9 %collective-permute-start.2 = (f32[1024,128]{1,0:T(8,128)S(1)}, f32[1024,128]{1,0:T(8,128)S(1)}, u32[]{:S(2)}, u32[]{:S(2)}) collective-permute-start(f32[1024,128]{1,0:T(8,128)S(1)} %fusion.61), channel_id=1, source_target_pairs={{0,1},{1,2},{2,3},{3,4},{4,5},{5,6},{6,7},{7,8},{8,9},{9,10},{10,1... | collective-permute-start | bytes 1572872 | tf_op jit(solution)/shard_map/while/body/eval_jaxpr/ppermute | solution.py:57
  122.3 14.8 %collective-permute-start = (bf16[1024,128]{1,0:T(8,128)(2,1)S(1)}, bf16[1024,128]{1,0:T(8,128)(2,1)S(1)}, u32[]{:S(2)}, u32[]{:S(2)}) collective-permute-start(bf16[1024,128]{1,0:T(8,128)(2,1)S(1)} %copy.12), channel_id=1, source_target_pairs={{0,1},{1,2},{2,3},{3,4},{4,5},{5,6},{6,7},{7,8},{8,9},{9,10},{10,1... | collective-permute-start | bytes 786440 | tf_op jit(solution)/shard_map/while/body/eval_jaxpr/ppermute | solution.py:55
  122.4 14.6 %collective-permute-start.1 = (f32[1024]{0:T(1024)S(1)}, f32[1024]{0:T(1024)S(1)}, u32[]{:S(2)}, u32[]{:S(2)}) collective-permute-start(f32[1024]{0:T(1024)S(1)} %copy.13), channel_id=1, source_target_pairs={{0,1},{1,2},{2,3},{3,4},{4,5},{5,6},{6,7},{7,8},{8,9},{9,10},{10,1... | collective-permute-start | bytes 12296 | tf_op jit(solution)/shard_map/while/body/eval_jaxpr/ppermute | solution.py:56
  141.6 14.9 %collective-permute-start.2 = (f32[1024,128]{1,0:T(8,128)S(1)}, f32[1024,128]{1,0:T(8,128)S(1)}, u32[]{:S(2)}, u32[]{:S(2)}) collective-permute-start(f32[1024,128]{1,0:T(8,128)S(1)} %fusion.61), channel_id=1, source_target_pairs={{0,1},{1,2},{2,3},{3,4},{4,5},{5,6},{6,7},{7,8},{8,9},{9,10},{10,1... | collective-permute-start | bytes 1572872 | tf_op jit(solution)/shard_map/while/body/eval_jaxpr/ppermute | solution.py:57
  141.7 14.8 %collective-permute-start = (bf16[1024,128]{1,0:T(8,128)(2,1)S(1)}, bf16[1024,128]{1,0:T(8,128)(2,1)S(1)}, u32[]{:S(2)}, u32[]{:S(2)}) collective-permute-start(bf16[1024,128]{1,0:T(8,128)(2,1)S(1)} %copy.12), channel_id=1, source_target_pairs={{0,1},{1,2},{2,3},{3,4},{4,5},{5,6},{6,7},{7,8},{8,9},{9,10},{10,1... | collective-permute-start | bytes 786440 | tf_op jit(solution)/shard_map/while/body/eval_jaxpr/ppermute | solution.py:55
  141.8 14.6 %collective-permute-start.1 = (f32[1024]{0:T(1024)S(1)}, f32[1024]{0:T(1024)S(1)}, u32[]{:S(2)}, u32[]{:S(2)}) collective-permute-start(f32[1024]{0:T(1024)S(1)} %copy.13), channel_id=1, source_target_pairs={{0,1},{1,2},{2,3},{3,4},{4,5},{5,6},{6,7},{7,8},{8,9},{9,10},{10,1... | collective-permute-start | bytes 12296 | tf_op jit(solution)/shard_map/while/body/eval_jaxpr/ppermute | solution.py:56
  161.0 14.9 %collective-permute-start.2 = (f32[1024,128]{1,0:T(8,128)S(1)}, f32[1024,128]{1,0:T(8,128)S(1)}, u32[]{:S(2)}, u32[]{:S(2)}) collective-permute-start(f32[1024,128]{1,0:T(8,128)S(1)} %fusion.61), channel_id=1, source_target_pairs={{0,1},{1,2},{2,3},{3,4},{4,5},{5,6},{6,7},{7,8},{8,9},{9,10},{10,1... | collective-permute-start | bytes 1572872 | tf_op jit(solution)/shard_map/while/body/eval_jaxpr/ppermute | solution.py:57
  161.1 14.8 %collective-permute-start = (bf16[1024,128]{1,0:T(8,128)(2,1)S(1)}, bf16[1024,128]{1,0:T(8,128)(2,1)S(1)}, u32[]{:S(2)}, u32[]{:S(2)}) collective-permute-start(bf16[1024,128]{1,0:T(8,128)(2,1)S(1)} %copy.12), channel_id=1, source_target_pairs={{0,1},{1,2},{2,3},{3,4},{4,5},{5,6},{6,7},{7,8},{8,9},{9,10},{10,1... | collective-permute-start | bytes 786440 | tf_op jit(solution)/shard_map/while/body/eval_jaxpr/ppermute | solution.py:55
  161.2 14.6 %collective-permute-start.1 = (f32[1024]{0:T(1024)S(1)}, f32[1024]{0:T(1024)S(1)}, u32[]{:S(2)}, u32[]{:S(2)}) collective-permute-start(f32[1024]{0:T(1024)S(1)} %copy.13), channel_id=1, source_target_pairs={{0,1},{1,2},{2,3},{3,4},{4,5},{5,6},{6,7},{7,8},{8,9},{9,10},{10,1... | collective-permute-start | bytes 12296 | tf_op jit(solution)/shard_map/while/body/eval_jaxpr/ppermute | solution.py:56
  180.4 14.9 %collective-permute-start.2 = (f32[1024,128]{1,0:T(8,128)S(1)}, f32[1024,128]{1,0:T(8,128)S(1)}, u32[]{:S(2)}, u32[]{:S(2)}) collective-permute-start(f32[1024,128]{1,0:T(8,128)S(1)} %fusion.61), channel_id=1, source_target_pairs={{0,1},{1,2},{2,3},{3,4},{4,5},{5,6},{6,7},{7,8},{8,9},{9,10},{10,1... | collective-permute-start | bytes 1572872 | tf_op jit(solution)/shard_map/while/body/eval_jaxpr/ppermute | solution.py:57
  180.5 14.8 %collective-permute-start = (bf16[1024,128]{1,0:T(8,128)(2,1)S(1)}, bf16[1024,128]{1,0:T(8,128)(2,1)S(1)}, u32[]{:S(2)}, u32[]{:S(2)}) collective-permute-start(bf16[1024,128]{1,0:T(8,128)(2,1)S(1)} %copy.12), channel_id=1, source_target_pairs={{0,1},{1,2},{2,3},{3,4},{4,5},{5,6},{6,7},{7,8},{8,9},{9,10},{10,1... | collective-permute-start | bytes 786440 | tf_op jit(solution)/shard_map/while/body/eval_jaxpr/ppermute | solution.py:55
  180.6 14.6 %collective-permute-start.1 = (f32[1024]{0:T(1024)S(1)}, f32[1024]{0:T(1024)S(1)}, u32[]{:S(2)}, u32[]{:S(2)}) collective-permute-start(f32[1024]{0:T(1024)S(1)} %copy.13), channel_id=1, source_target_pairs={{0,1},{1,2},{2,3},{3,4},{4,5},{5,6},{6,7},{7,8},{8,9},{9,10},{10,1... | collective-permute-start | bytes 12296 | tf_op jit(solution)/shard_map/while/body/eval_jaxpr/ppermute | solution.py:56
  199.8 14.9 %collective-permute-start.2 = (f32[1024,128]{1,0:T(8,128)S(1)}, f32[1024,128]{1,0:T(8,128)S(1)}, u32[]{:S(2)}, u32[]{:S(2)}) collective-permute-start(f32[1024,128]{1,0:T(8,128)S(1)} %fusion.61), channel_id=1, source_target_pairs={{0,1},{1,2},{2,3},{3,4},{4,5},{5,6},{6,7},{7,8},{8,9},{9,10},{10,1... | collective-permute-start | bytes 1572872 | tf_op jit(solution)/shard_map/while/body/eval_jaxpr/ppermute | solution.py:57
  199.9 14.8 %collective-permute-start = (bf16[1024,128]{1,0:T(8,128)(2,1)S(1)}, bf16[1024,128]{1,0:T(8,128)(2,1)S(1)}, u32[]{:S(2)}, u32[]{:S(2)}) collective-permute-start(bf16[1024,128]{1,0:T(8,128)(2,1)S(1)} %copy.12), channel_id=1, source_target_pairs={{0,1},{1,2},{2,3},{3,4},{4,5},{5,6},{6,7},{7,8},{8,9},{9,10},{10,1... | collective-permute-start | bytes 786440 | tf_op jit(solution)/shard_map/while/body/eval_jaxpr/ppermute | solution.py:55
  200.0 14.6 %collective-permute-start.1 = (f32[1024]{0:T(1024)S(1)}, f32[1024]{0:T(1024)S(1)}, u32[]{:S(2)}, u32[]{:S(2)}) collective-permute-start(f32[1024]{0:T(1024)S(1)} %copy.13), channel_id=1, source_target_pairs={{0,1},{1,2},{2,3},{3,4},{4,5},{5,6},{6,7},{7,8},{8,9},{9,10},{10,1... | collective-permute-start | bytes 12296 | tf_op jit(solution)/shard_map/while/body/eval_jaxpr/ppermute | solution.py:56
  219.2 14.9 %collective-permute-start.2 = (f32[1024,128]{1,0:T(8,128)S(1)}, f32[1024,128]{1,0:T(8,128)S(1)}, u32[]{:S(2)}, u32[]{:S(2)}) collective-permute-start(f32[1024,128]{1,0:T(8,128)S(1)} %fusion.61), channel_id=1, source_target_pairs={{0,1},{1,2},{2,3},{3,4},{4,5},{5,6},{6,7},{7,8},{8,9},{9,10},{10,1... | collective-permute-start | bytes 1572872 | tf_op jit(solution)/shard_map/while/body/eval_jaxpr/ppermute | solution.py:57
  219.3 14.8 %collective-permute-start = (bf16[1024,128]{1,0:T(8,128)(2,1)S(1)}, bf16[1024,128]{1,0:T(8,128)(2,1)S(1)}, u32[]{:S(2)}, u32[]{:S(2)}) collective-permute-start(bf16[1024,128]{1,0:T(8,128)(2,1)S(1)} %copy.12), channel_id=1, source_target_pairs={{0,1},{1,2},{2,3},{3,4},{4,5},{5,6},{6,7},{7,8},{8,9},{9,10},{10,1... | collective-permute-start | bytes 786440 | tf_op jit(solution)/shard_map/while/body/eval_jaxpr/ppermute | solution.py:55
  219.4 14.6 %collective-permute-start.1 = (f32[1024]{0:T(1024)S(1)}, f32[1024]{0:T(1024)S(1)}, u32[]{:S(2)}, u32[]{:S(2)}) collective-permute-start(f32[1024]{0:T(1024)S(1)} %copy.13), channel_id=1, source_target_pairs={{0,1},{1,2},{2,3},{3,4},{4,5},{5,6},{6,7},{7,8},{8,9},{9,10},{10,1... | collective-permute-start | bytes 12296 | tf_op jit(solution)/shard_map/while/body/eval_jaxpr/ppermute | solution.py:56
  238.6 14.9 %collective-permute-start.2 = (f32[1024,128]{1,0:T(8,128)S(1)}, f32[1024,128]{1,0:T(8,128)S(1)}, u32[]{:S(2)}, u32[]{:S(2)}) collective-permute-start(f32[1024,128]{1,0:T(8,128)S(1)} %fusion.61), channel_id=1, source_target_pairs={{0,1},{1,2},{2,3},{3,4},{4,5},{5,6},{6,7},{7,8},{8,9},{9,10},{10,1... | collective-permute-start | bytes 1572872 | tf_op jit(solution)/shard_map/while/body/eval_jaxpr/ppermute | solution.py:57
  238.7 14.8 %collective-permute-start = (bf16[1024,128]{1,0:T(8,128)(2,1)S(1)}, bf16[1024,128]{1,0:T(8,128)(2,1)S(1)}, u32[]{:S(2)}, u32[]{:S(2)}) collective-permute-start(bf16[1024,128]{1,0:T(8,128)(2,1)S(1)} %copy.12), channel_id=1, source_target_pairs={{0,1},{1,2},{2,3},{3,4},{4,5},{5,6},{6,7},{7,8},{8,9},{9,10},{10,1... | collective-permute-start | bytes 786440 | tf_op jit(solution)/shard_map/while/body/eval_jaxpr/ppermute | solution.py:55
  238.8 14.6 %collective-permute-start.1 = (f32[1024]{0:T(1024)S(1)}, f32[1024]{0:T(1024)S(1)}, u32[]{:S(2)}, u32[]{:S(2)}) collective-permute-start(f32[1024]{0:T(1024)S(1)} %copy.13), channel_id=1, source_target_pairs={{0,1},{1,2},{2,3},{3,4},{4,5},{5,6},{6,7},{7,8},{8,9},{9,10},{10,1... | collective-permute-start | bytes 12296 | tf_op jit(solution)/shard_map/while/body/eval_jaxpr/ppermute | solution.py:56
  258.0 14.9 %collective-permute-start.2 = (f32[1024,128]{1,0:T(8,128)S(1)}, f32[1024,128]{1,0:T(8,128)S(1)}, u32[]{:S(2)}, u32[]{:S(2)}) collective-permute-start(f32[1024,128]{1,0:T(8,128)S(1)} %fusion.61), channel_id=1, source_target_pairs={{0,1},{1,2},{2,3},{3,4},{4,5},{5,6},{6,7},{7,8},{8,9},{9,10},{10,1... | collective-permute-start | bytes 1572872 | tf_op jit(solution)/shard_map/while/body/eval_jaxpr/ppermute | solution.py:57
  258.1 14.8 %collective-permute-start = (bf16[1024,128]{1,0:T(8,128)(2,1)S(1)}, bf16[1024,128]{1,0:T(8,128)(2,1)S(1)}, u32[]{:S(2)}, u32[]{:S(2)}) collective-permute-start(bf16[1024,128]{1,0:T(8,128)(2,1)S(1)} %copy.12), channel_id=1, source_target_pairs={{0,1},{1,2},{2,3},{3,4},{4,5},{5,6},{6,7},{7,8},{8,9},{9,10},{10,1... | collective-permute-start | bytes 786440 | tf_op jit(solution)/shard_map/while/body/eval_jaxpr/ppermute | solution.py:55
  258.2 14.6 %collective-permute-start.1 = (f32[1024]{0:T(1024)S(1)}, f32[1024]{0:T(1024)S(1)}, u32[]{:S(2)}, u32[]{:S(2)}) collective-permute-start(f32[1024]{0:T(1024)S(1)} %copy.13), channel_id=1, source_target_pairs={{0,1},{1,2},{2,3},{3,4},{4,5},{5,6},{6,7},{7,8},{8,9},{9,10},{10,1... | collective-permute-start | bytes 12296 | tf_op jit(solution)/shard_map/while/body/eval_jaxpr/ppermute | solution.py:56
  277.4 14.9 %collective-permute-start.2 = (f32[1024,128]{1,0:T(8,128)S(1)}, f32[1024,128]{1,0:T(8,128)S(1)}, u32[]{:S(2)}, u32[]{:S(2)}) collective-permute-start(f32[1024,128]{1,0:T(8,128)S(1)} %fusion.61), channel_id=1, source_target_pairs={{0,1},{1,2},{2,3},{3,4},{4,5},{5,6},{6,7},{7,8},{8,9},{9,10},{10,1... | collective-permute-start | bytes 1572872 | tf_op jit(solution)/shard_map/while/body/eval_jaxpr/ppermute | solution.py:57
  277.5 14.8 %collective-permute-start = (bf16[1024,128]{1,0:T(8,128)(2,1)S(1)}, bf16[1024,128]{1,0:T(8,128)(2,1)S(1)}, u32[]{:S(2)}, u32[]{:S(2)}) collective-permute-start(bf16[1024,128]{1,0:T(8,128)(2,1)S(1)} %copy.12), channel_id=1, source_target_pairs={{0,1},{1,2},{2,3},{3,4},{4,5},{5,6},{6,7},{7,8},{8,9},{9,10},{10,1... | collective-permute-start | bytes 786440 | tf_op jit(solution)/shard_map/while/body/eval_jaxpr/ppermute | solution.py:55
  277.6 14.6 %collective-permute-start.1 = (f32[1024]{0:T(1024)S(1)}, f32[1024]{0:T(1024)S(1)}, u32[]{:S(2)}, u32[]{:S(2)}) collective-permute-start(f32[1024]{0:T(1024)S(1)} %copy.13), channel_id=1, source_target_pairs={{0,1},{1,2},{2,3},{3,4},{4,5},{5,6},{6,7},{7,8},{8,9},{9,10},{10,1... | collective-permute-start | bytes 12296 | tf_op jit(solution)/shard_map/while/body/eval_jaxpr/ppermute | solution.py:56
  295.5 62.2 %collective-permute-start.5 = (f32[1024,128]{1,0:T(8,128)S(1)}, f32[1024,128]{1,0:T(8,128)S(1)}, u32[]{:S(2)}, u32[]{:S(2)}) collective-permute-start(f32[1024,128]{1,0:T(8,128)S(1)} %select_add_fusion), channel_id=1, source_target_pairs={{0,16},{1,17},{2,18},{3,19},{4,20},{5,21},{6,22},{7,23},{8,24},{9,... | collective-permute-start | bytes 1572872 | tf_op jit(solution)/shard_map/ppermute | solution.py:75
  (2 other events, 285.3 us)
where the time goes:
time: 359 us
  waiting for transfers between devices  173 us (48%)
  matrix products  80.5 us (22%)
  blocking collectives  61.4 us (17%)
  starting transfers between devices  20.9 us (6%)
  loops' own time  11.2 us (3%)
  other arithmetic  8.33 us (2%)
    ppermute x15, waiting for transfers between devices, full_step(): vis_q = lax.ppermute(vis_q, 'row', next_perm)  173 us
    psum x1, blocking collectives, per_device(): energy = lax.psum(energy, 'row')  61.4 us
    dot_general x17, matrix products, pair_weight(): jnp.einsum('id,jd->ij', row_pos, col_pos, preferred_element_type=jnp.floa...  56.2 us
    dot_general x17, matrix products, row_force(): pulled = jnp.dot(w_low, col_pos, preferred_element_type=jnp.float32)  12.3 us
    dot_general x16, matrix products, col_force(): jnp.einsum('ij,id->jd', w_low, row_pos, preferred_element_type=jnp.float32)  12 us
    another operation x1, loops' own time, per_device(): lax.fori_loop(0, half_way - 1, full_step, (vis_pos, vis_q, vis_react, own...  11.2 us
    ppermute x15, starting transfers between devices, full_step(): vis_react = lax.ppermute(vis_react, 'row', next_perm)  10 us
  transfers between devices with their start and end apart: 48, of which 15 were waited for; matrix products, arithmetic and copies ran while one was open for 5% of the time, Pallas kernels for 0%

commit v1 on v0

v1 whole, which is shorter than its diff:
```python
import functools
import math

import jax
import jax.numpy as jnp
from jax import lax
from jax.experimental import pallas as pl
from jax.experimental.pallas import tpu as pltpu
from jax.sharding import PartitionSpec as P

MESH = pl.DeviceIdType.MESH
BF16, F32 = jnp.bfloat16, jnp.float32
TILE = 256
AUG = 16
S_CAP = 1.69e38
C_CAP = 3.3895313892515355e38


def split3(val):
    hi = jnp.clip(val, -C_CAP, C_CAP).astype(BF16).astype(F32)
    mid = (val - hi).astype(BF16).astype(F32)
    low = (val - hi - mid).astype(BF16).astype(F32)
    return hi, mid, low


def dot(lhs, rhs, dims):
    return lax.dot_general(lhs, rhs, (dims, ((), ())), preferred_element_type=F32)


def stage_list(side):
    far = side // 2
    assert side == 4
    return [(0, 1), (0, -1), (1, 0), (-1, 0), (0, far), (1, 1), (1, -1), (-1, 1), (-1, -1), (far, 0),
            (1, far), (-1, far), (far, 1), (far, -1), (far, far)]


def kernel(side, width, x_ref, q_ref, cnt_ref, out_ref, e_ref, slots, xa, ci, s_acc, t_acc, ebuf,
           send_sem, recv_sem, dsend_sem, drecv_sem, esend_sem, erecv_sem):
    rows = x_ref.shape[0]
    n_tiles = rows // TILE
    half = n_tiles // 2
    n_dev = 2 * side * side
    me = lax.axis_index('row')
    sys_id = lax.axis_index('sys')
    core = lax.rem(me, 2)
    chip = lax.div(me, 2)
    pos_y, pos_x = lax.div(chip, side), lax.rem(chip, side)
    stages = stage_list(side)
    scale = math.log2(math.e) / width

    def dev(dy, dx, plane):
        return (lax.rem(pos_y + dy + side, side) * side + lax.rem(pos_x + dx + side, side)) * 2 + plane

    mate = me + 1 - 2 * core
    barrier = pltpu.get_barrier_semaphore()

    def greet(step, carry):
        pl.semaphore_signal(barrier, inc=1, device_id=(sys_id, lax.rem(me + step, n_dev)), device_id_type=MESH)
        return carry
    lax.fori_loop(1, n_dev, greet, 0)

    count = cnt_ref[0]
    row_id = lax.broadcasted_iota(jnp.int32, (rows, width), 0)
    lane_id = lax.broadcasted_iota(jnp.int32, (rows, width), 1)
    x_val = jnp.where(row_id < count, x_ref[...].astype(F32), 0.0)
    x_t = x_val.T
    s_row = -jnp.minimum(0.5 * jnp.sum(x_t * x_t, axis=0, keepdims=True), S_CAP)
    s_col = -jnp.minimum(0.5 * jnp.sum(x_val * x_val, axis=1, keepdims=True), S_CAP)
    q_shape = q_ref.shape
    q_id = lax.broadcasted_iota(jnp.int32, q_shape, 0) * q_shape[1] + lax.broadcasted_iota(jnp.int32, q_shape, 1)
    q_val = jnp.where(q_id < count, q_ref[...], 0.0)
    q_row = jnp.concatenate([q_val[r:r + 1, :] for r in range(q_shape[0])], axis=1)
    aug_id = lax.broadcasted_iota(jnp.int32, (AUG, rows), 0)
    aug = jnp.where(aug_id < 3, 1.0, 0.0)
    for k, part in enumerate(split3(s_row) + split3(q_row)):
        aug = jnp.where(aug_id == 3 + k, part, aug)
    for t in range(n_tiles):
        cols = slice(t * TILE, (t + 1) * TILE)
        slots[me * n_tiles + t, :width, :] = x_t[:, cols].astype(BF16)
        slots[me * n_tiles + t, width:, :] = aug[:, cols].astype(BF16)
    xa[:, :width] = x_val.astype(BF16)
    tail = jnp.where((lane_id >= 3) & (lane_id < 6), 1.0, 0.0)
    for k, part in enumerate(split3(s_col)):
        tail = jnp.where(lane_id == k, part, tail)
    xa[:, width:] = tail.astype(BF16)
    q_t = q_val.T
    for r in range(q_shape[0]):
        lanes = q_shape[1]
        ci[r * lanes:(r + 1) * lanes, :] = jnp.broadcast_to(q_t[:, r:r + 1], (lanes, width))
    s_acc[...] = jnp.zeros_like(s_acc)
    t_acc[...] = jnp.zeros_like(t_acc)

    pl.semaphore_wait(barrier, n_dev - 1)

    def wrap(d):
        return (d + 1) % side - 1
    stage_of = {d: k for k, d in enumerate(stages)}
    sends = []

    def stage_disp(k, t):
        dy, dx = stages[k]
        return (dy, dx) if t < half else (dx, dy)

    def make_send(disp, t, hop, idx):
        dy, dx = wrap(disp[0] - hop[0]), wrap(disp[1] - hop[1])
        k = stage_of[(dy, dx) if t < half else (dx, dy)]
        unit = dev(disp[0], disp[1], core) * n_tiles + t
        return pltpu.make_async_remote_copy(
            src_ref=slots.at[unit], dst_ref=slots.at[unit], send_sem=send_sem.at[idx], recv_sem=recv_sem.at[k, t],
            device_id=(sys_id, dev(hop[0], hop[1], core)), device_id_type=MESH)

    def flip(pair, t):
        return pair if t < half else (pair[1], pair[0])

    def relays(k):
        found = []
        slow, fast = (0, 0) if k < 0 else stages[k]
        for t in range(n_tiles):
            first = t % half == 0
            if k < 0:
                found += [((0, 0), t, flip((0, sgn), t)) for sgn in (1, -1)]
            elif slow == 0 and abs(fast) == 1 and first == (fast == 1):
                found.append((flip((slow, fast), t), t, flip((0, -fast), t)))
        for t in range(n_tiles):
            first = t % half == 0
            if slow == 0:
                found += [(flip((slow, fast), t), t, flip((sgn, 0), t)) for sgn in (1, -1)]
            elif abs(slow) == 1 and first == (slow == 1):
                found.append((flip((slow, fast), t), t, flip((-slow, 0), t)))
        return found

    def start_relays(k):
        for disp, t, hop in relays(k):
            make_send(disp, t, hop, len(sends)).start()
            sends.append(0)

    def mate_copy(k, part):
        dy, dx = (0, 0) if k < 0 else stage_disp(k, part * half)
        unit = dev(dy, dx, core) * n_tiles + part * half
        return pltpu.make_async_remote_copy(
            src_ref=slots.at[pl.ds(unit, half)], dst_ref=slots.at[pl.ds(unit, half)],
            send_sem=dsend_sem.at[k + 1, part], recv_sem=drecv_sem.at[k + 1, part],
            device_id=(sys_id, mate), device_id_type=MESH)

    def mate_recv(k, part):
        dy, dx = (0, 0) if k < 0 else stage_disp(k, part * half)
        unit = dev(dy, dx, 1 - core) * n_tiles + part * half
        return pltpu.make_async_remote_copy(
            src_ref=slots.at[pl.ds(unit, half)], dst_ref=slots.at[pl.ds(unit, half)],
            send_sem=dsend_sem.at[k + 1, part], recv_sem=drecv_sem.at[k + 1, part],
            device_id=(sys_id, mate), device_id_type=MESH)

    def recv(k, t):
        dy, dx = stage_disp(k, t)
        unit = dev(dy, dx, core) * n_tiles + t
        return pltpu.make_async_remote_copy(
            src_ref=slots.at[unit], dst_ref=slots.at[unit], send_sem=send_sem.at[0], recv_sem=recv_sem.at[k, t],
            device_id=(sys_id, mate), device_id_type=MESH)

    eye = (lax.broadcasted_iota(jnp.int32, (TILE, TILE), 0) == lax.broadcasted_iota(jnp.int32, (TILE, TILE), 1))
    pad = jnp.zeros((2 * width - width - AUG, TILE), BF16)

    def column_tile(unit, diag=None):
        block = slots[unit]
        aug_rhs = jnp.concatenate([block, pad], axis=0)
        parts = block[width:, :].astype(F32)
        cj = parts[6:7, :] + parts[7:8, :] + parts[8:9, :]
        for it in range(n_tiles):
            mine = slice(it * TILE, (it + 1) * TILE)
            arg = dot(xa[mine, :], aug_rhs, ((1,), (0,)))
            weight = jnp.exp2(jnp.minimum(arg, 0.0) * scale) * cj
            if it == diag:
                weight = jnp.where(eye, 0.0, weight)
            c_mine = ci[mine, :]
            left, right = weight[:, :width] * c_mine, weight[:, width:] * c_mine
            s_acc[mine, :] += left + right
            w_low = jnp.concatenate([left, right], axis=1).astype(BF16)
            t_acc[mine, :] += dot(w_low, block[:width, :], ((1,), (1,)))

    start_relays(-1)
    for part in range(2):
        mate_copy(-1, part).start()
    for t in range(n_tiles):
        column_tile(me * n_tiles + t, diag=t)

    def base_unit(step, part, plane):
        dy, dx = jnp.int32(0), jnp.int32(0)
        for k in range(len(stages)):
            sy, sx = stage_disp(k, part * half)
            dy = jnp.where(step == k, sy, dy)
            dx = jnp.where(step == k, sx, dx)
        return dev(dy, dx, plane) * n_tiles + part * half

    def step_body(step, carry):
        for k in range(len(stages)):
            @pl.when(step == k)
            def _():
                for t in range(n_tiles):
                    recv(k, t).wait_recv()
                start_relays(k)
                for part in range(2):
                    mate_copy(k, part).start()
                for part in range(2):
                    mate_recv(k - 1, part).wait_recv()
        for part in range(2):
            unit = base_unit(step, part, core)
            for t in range(half):
                column_tile(unit + t)
        for part in range(2):
            unit = base_unit(step - 1, part, 1 - core)
            for t in range(half):
                column_tile(unit + t)
        return carry
    lax.fori_loop(0, len(stages), step_body, 0)
    last = len(stages) - 1
    for part in range(2):
        mate_recv(last, part).wait_recv()
    for part in range(2):
        unit = base_unit(last, part, 1 - core)
        for t in range(half):
            column_tile(unit + t)

    s_sum = jnp.sum(s_acc[...], axis=1, keepdims=True)
    x_own = xa[:, :width].astype(F32)
    out_ref[...] = (s_sum * x_own - t_acc[...]) * (1.0 / width)
    ebuf[me] = jnp.sum(s_acc[...].reshape(rows // 8, 8, width), axis=0)

    def e_copy(step):
        return pltpu.make_async_remote_copy(
            src_ref=ebuf.at[me], dst_ref=ebuf.at[me], send_sem=esend_sem.at[step], recv_sem=erecv_sem.at[me],
            device_id=(sys_id, lax.rem(me + step, n_dev)), device_id_type=MESH)

    def e_start(step, carry):
        e_copy(step).start()
        return carry
    lax.fori_loop(1, n_dev, e_start, 0)

    def e_wait(step, carry):
        src = lax.rem(me + step, n_dev)
        pltpu.make_async_remote_copy(
            src_ref=ebuf.at[src], dst_ref=ebuf.at[src], send_sem=esend_sem.at[step], recv_sem=erecv_sem.at[src],
            device_id=(sys_id, mate), device_id_type=MESH).wait_recv()
        return carry
    lax.fori_loop(1, n_dev, e_wait, 0)
    e_ref[0] = 0.5 * jnp.sum(ebuf[...])

    def e_sent(step, carry):
        e_copy(step).wait_send()
        return carry
    lax.fori_loop(1, n_dev, e_sent, 0)

    def sent(idx, carry):
        pltpu.make_async_remote_copy(
            src_ref=slots.at[0], dst_ref=slots.at[0], send_sem=send_sem.at[idx], recv_sem=recv_sem.at[0, 0],
            device_id=(sys_id, mate), device_id_type=MESH).wait_send()
        return carry
    lax.fori_loop(0, len(sends), sent, 0)
    for k in range(-1, len(stages)):
        for part in range(2):
            mate_copy(k, part).wait_send()


def solution(mesh):
    n_dev = mesh.shape['row']
    side = math.isqrt(n_dev // 2)

    def per_device(positions, charges, counts):
        rows, width = positions.shape
        n_tiles = rows // TILE
        n_stages = len(stage_list(side))
        n_sends = n_tiles * n_stages
        vmem = pl.BlockSpec(memory_space=pltpu.VMEM)
        smem = pl.BlockSpec(memory_space=pltpu.SMEM)
        force, energy = pl.pallas_call(
            functools.partial(kernel, side, width),
            out_shape=[jax.ShapeDtypeStruct((rows, width), F32), jax.ShapeDtypeStruct((1,), F32)],
            in_specs=[vmem, vmem, smem],
            out_specs=[vmem, smem],
            scratch_shapes=[
                pltpu.VMEM((n_dev * n_tiles, width + AUG, TILE), BF16),
                pltpu.VMEM((rows, 2 * width), BF16),
                pltpu.VMEM((rows, width), F32),
                pltpu.VMEM((rows, width), F32),
                pltpu.VMEM((rows, width), F32),
                pltpu.VMEM((n_dev, 8, width), F32),
                pltpu.SemaphoreType.DMA((n_sends,)),
                pltpu.SemaphoreType.DMA((n_stages, n_tiles)),
                pltpu.SemaphoreType.DMA((n_stages + 1, 2)),
                pltpu.SemaphoreType.DMA((n_stages + 1, 2)),
                pltpu.SemaphoreType.DMA((n_dev,)),
                pltpu.SemaphoreType.DMA((n_dev,)),
            ],
            compiler_params=pltpu.CompilerParams(collective_id=0, has_side_effects=True, vmem_limit_bytes=48 * 2 ** 20),
            name='pair_forces',
        )(positions, charges.reshape(rows // width, width), counts)
        return force, energy

    row_spec = P(('sys', 'row'), None)
    vec_spec = P(('sys', 'row'))
    return jax.shard_map(per_device, mesh=mesh, in_specs=(row_spec, vec_spec, vec_spec),
                         out_specs=(row_spec, P('sys')), check_vma=False)
```

time: 359 us -> 69.9 us (0.19)
  waiting for transfers between devices: 173 us -> 0 us
  matrix products: 80.5 us -> 0 us
  Pallas kernels: 0 us -> 64.2 us
  blocking collectives: 61.4 us -> 0 us
  starting transfers between devices: 20.9 us -> 0 us
  loops' own time: 11.2 us -> 0 us
  other arithmetic: 8.33 us -> 0 us
    ppermute x48 -> x0, waiting for transfers between devices: 173 us -> none  [the longest x15 173 us: full_step(): vis_q = lax.ppermute(vis_q, 'row', next_perm)]
    dot_general x50 -> x0, matrix products: 80.5 us -> none  [the longest x17 56.2 us: pair_weight(): jnp.einsum('id,jd->ij', row_pos, col_pos, preferred_element_type=jnp.floa...]
    pallas_call x0 -> x1, Pallas kernels: none -> 64.2 us  [per_device(): pl.pallas_call(functools.partial(kernel, side, width), out_shape=[jax.Sha...]
    psum x1 -> x0, blocking collectives: 61.4 us -> none  [per_device(): energy = lax.psum(energy, 'row')]
    ppermute x48 -> x0, starting transfers between devices: 20.9 us -> none  [the longest x15 10 us: full_step(): vis_react = lax.ppermute(vis_react, 'row', next_perm)]
    another operation x1 -> x0, loops' own time: 11.2 us -> none  [per_device(): lax.fori_loop(0, half_way - 1, full_step, (vis_pos, vis_q, vis_react, own...]
    reduce_sum x18 -> x0, other arithmetic: 6.68 us -> none  [sq_norm(): return jnp.sum(pos_f32 * pos_f32, axis=1)]
  transfers between devices with their start and end apart: 48 -> 0, of which waited for: 15 -> 0; matrix products, arithmetic and copies ran while one was open for 5% -> 0% of each run, Pallas kernels for 0% -> 0%
where the time goes in v1:
time: 69.9 us; the launch traced here: 69.7 us
  Pallas kernels  64.2 us (92%)
  between operations  3.06 us (4%)
  local copies, waits for them, and re-layouts  2.43 us (3%)
    pallas_call x1, Pallas kernels, per_device(): pl.pallas_call(functools.partial(kernel, side, width), out_shape=[jax.Sha...  64.2 us
    unnamed x5, local copies, waits for them, and re-layouts  2.43 us

profile of v1, /device:TPU:97, one launch (start us, length us, event | category | flops | bytes accessed | tf_op | source)
XLA Modules:
  0.0 69.7 jit_solution(13035492579016322157)
XLA Ops:
  1.3 0.0 copy-start
  1.3 0.9 %copy-done = bf16[1024,128]{1,0:T(8,128)(2,1)S(1)} copy-done((bf16[1024,128]{1,0:T(8,128)(2,1)S(1)}, bf16[1024,128]{1,0:T(8,128)(2,1)}, u32[]{:S(2)}) %copy-start) | copy-done | bytes 262168
  2.2 0.0 copy-start.1
  2.2 0.7 copy-done.1
  2.9 64.2 %pair_forces.1 = (f32[1024,128]{1,0:T(8,128)S(1)}, f32[1]{0:T(128)}) custom-call(bf16[1024,128]{1,0:T(8,128)(2,1)S(1)} %copy-done, f32[8,128]{1,0:T(8,128)S(1)} %bitcast.1, s32[1]{0:T(128)S(6)} %copy.7.cnt_ref), custom_call_target="tpu_custom_call" | custom-call | tf_op jit(solution)/shard_map/pair_forces/pallas_call | solution.py:274
  67.1 0.8 %copy.8 = f32[1024,128]{1,0:T(8,128)} copy(f32[1024,128]{1,0:T(8,128)S(1)} %get-tuple-element.4) | data formatting | bytes 1048576
Async XLA Ops:
  1.3 1.0 %copy-start = (bf16[1024,128]{1,0:T(8,128)(2,1)S(1)}, bf16[1024,128]{1,0:T(8,128)(2,1)}, u32[]{:S(2)}) copy-start(bf16[1024,128]{1,0:T(8,128)(2,1)} %x_ref.1) | copy-start | bytes 786436
  2.2 0.7 copy-start.1

commit v2 on v1

--- a/solution.py
+++ b/solution.py
@@ -34,8 +34,18 @@
             (1, far), (-1, far), (far, 1), (far, -1), (far, far)]
 
 
-def kernel(side, width, x_ref, q_ref, cnt_ref, out_ref, e_ref, slots, xa, ci, s_acc, t_acc, ebuf,
+ARRIVALS = {-1: (0,), 0: (1,), 1: (2,), 2: (3,), 3: (4,), 4: (5, 6), 5: (7, 8), 6: (10, 11), 7: (9,), 8: (12,), 9: (14, 13)}
+COMPUTE = (0, 1, 2, 3, 4, 5, 6, 7, 10, 9, 12, 14, 8, 11, 13)
+SHARE = (1.0, 0.0, 1.0, 0.0, 0.5, 1.0, 0.5, 0.5, 0.0, 0.5, 1.0, 0.0, 1.0, 0.0, 0.5)
+ENERGY_STEP = 12
+
+
+def kernel(side, width, x_hbm, q_hbm, cnt_ref, out_ref, e_ref, x_ref, q_ref, in_sem, slots, xa, ci, s_acc, t_acc, ebuf,
            send_sem, recv_sem, dsend_sem, drecv_sem, esend_sem, erecv_sem):
+    x_in = pltpu.make_async_copy(x_hbm, x_ref, in_sem.at[0])
+    q_in = pltpu.make_async_copy(q_hbm, q_ref, in_sem.at[1])
+    x_in.start()
+    q_in.start()
     rows = x_ref.shape[0]
     n_tiles = rows // TILE
     half = n_tiles // 2
@@ -54,10 +64,11 @@
     mate = me + 1 - 2 * core
     barrier = pltpu.get_barrier_semaphore()
 
-    def greet(step, carry):
-        pl.semaphore_signal(barrier, inc=1, device_id=(sys_id, lax.rem(me + step, n_dev)), device_id_type=MESH)
-        return carry
-    lax.fori_loop(1, n_dev, greet, 0)
+    near = [dev(0, 1, core), dev(0, -1, core), dev(1, 0, core), dev(-1, 0, core), mate]
+    for peer in near:
+        pl.semaphore_signal(barrier, inc=1, device_id=(sys_id, peer), device_id_type=MESH)
+    x_in.wait()
+    q_in.wait()
 
     count = cnt_ref[0]
     row_id = lax.broadcasted_iota(jnp.int32, (rows, width), 0)
@@ -90,7 +101,7 @@
     s_acc[...] = jnp.zeros_like(s_acc)
     t_acc[...] = jnp.zeros_like(t_acc)
 
-    pl.semaphore_wait(barrier, n_dev - 1)
+    pl.semaphore_wait(barrier, len(near))
 
     def wrap(d):
         return (d + 1) % side - 1
@@ -185,56 +196,62 @@
 
     def base_unit(step, part, plane):
         dy, dx = jnp.int32(0), jnp.int32(0)
-        for k in range(len(stages)):
-            sy, sx = stage_disp(k, part * half)
-            dy = jnp.where(step == k, sy, dy)
-            dx = jnp.where(step == k, sx, dx)
+        for now in range(len(stages)):
+            sy, sx = stage_disp(COMPUTE[now], part * half)
+            dy = jnp.where(step == now, sy, dy)
+            dx = jnp.where(step == now, sx, dx)
         return dev(dy, dx, plane) * n_tiles + part * half
 
+    def arrive(k):
+        for t in range(n_tiles):
+            recv(k, t).wait_recv()
+        start_relays(k)
+        for part in range(2):
+            mate_copy(k, part).start()
+
+    def e_copy(step):
+        return pltpu.make_async_remote_copy(
+            src_ref=ebuf.at[me], dst_ref=ebuf.at[me], send_sem=esend_sem.at[step], recv_sem=erecv_sem.at[me],
+            device_id=(sys_id, lax.rem(me + step, n_dev)), device_id_type=MESH)
+
+    def e_start(step, carry):
+        e_copy(step).start()
+        return carry
+
+    def tally(weight):
+        ebuf[me] += weight * jnp.sum(s_acc[...].reshape(rows // 8, 8, width), axis=0)
+
+    arrive(ARRIVALS[-1][0])
+    for part in range(2):
+        mate_recv(-1, part).wait_recv()
+    ebuf[me] = jnp.zeros(ebuf.shape[1:], F32)
+    for t in range(n_tiles):
+        column_tile((mate * n_tiles) + t)
+    share = [0.5] + [SHARE[k] for k in COMPUTE]
+
     def step_body(step, carry):
-        for k in range(len(stages)):
-            @pl.when(step == k)
+        for now in range(len(stages)):
+            @pl.when(step == now)
             def _():
-                for t in range(n_tiles):
-                    recv(k, t).wait_recv()
-                start_relays(k)
+                for k in ARRIVALS.get(now, ()):
+                    arrive(k)
                 for part in range(2):
-                    mate_copy(k, part).start()
-                for part in range(2):
-                    mate_recv(k - 1, part).wait_recv()
+                    mate_recv(COMPUTE[now], part).wait_recv()
+                if now <= ENERGY_STEP and share[now] != share[now + 1]:
+                    tally(share[now] - share[now + 1])
+                if now == ENERGY_STEP:
+                    lax.fori_loop(1, n_dev, e_start, 0)
         for part in range(2):
-            unit = base_unit(step, part, core)
-            for t in range(half):
-                column_tile(unit + t)
-        for part in range(2):
-            unit = base_unit(step - 1, part, 1 - core)
-            for t in range(half):
-                column_tile(unit + t)
+            for plane in (core, 1 - core):
+                unit = base_unit(step, part, plane)
+                for t in range(half):
+                    column_tile(unit + t)
         return carry
     lax.fori_loop(0, len(stages), step_body, 0)
-    last = len(stages) - 1
-    for part in range(2):
-        mate_recv(last, part).wait_recv()
-    for part in range(2):
-        unit = base_unit(last, part, 1 - core)
-        for t in range(half):
-            column_tile(unit + t)
 
     s_sum = jnp.sum(s_acc[...], axis=1, keepdims=True)
     x_own = xa[:, :width].astype(F32)
     out_ref[...] = (s_sum * x_own - t_acc[...]) * (1.0 / width)
-    ebuf[me] = jnp.sum(s_acc[...].reshape(rows // 8, 8, width), axis=0)
-
-    def e_copy(step):
-        return pltpu.make_async_remote_copy(
-            src_ref=ebuf.at[me], dst_ref=ebuf.at[me], send_sem=esend_sem.at[step], recv_sem=erecv_sem.at[me],
-            device_id=(sys_id, lax.rem(me + step, n_dev)), device_id_type=MESH)
-
-    def e_start(step, carry):
-        e_copy(step).start()
-        return carry
-    lax.fori_loop(1, n_dev, e_start, 0)
-
     def e_wait(step, carry):
         src = lax.rem(me + step, n_dev)
         pltpu.make_async_remote_copy(
@@ -242,7 +259,7 @@
             device_id=(sys_id, mate), device_id_type=MESH).wait_recv()
         return carry
     lax.fori_loop(1, n_dev, e_wait, 0)
-    e_ref[0] = 0.5 * jnp.sum(ebuf[...])
+    e_ref[0] = jnp.sum(ebuf[...])
 
     def e_sent(step, carry):
         e_copy(step).wait_send()
@@ -271,12 +288,16 @@
         n_sends = n_tiles * n_stages
         vmem = pl.BlockSpec(memory_space=pltpu.VMEM)
         smem = pl.BlockSpec(memory_space=pltpu.SMEM)
+        hbm = pl.BlockSpec(memory_space=pl.ANY)
         force, energy = pl.pallas_call(
             functools.partial(kernel, side, width),
             out_shape=[jax.ShapeDtypeStruct((rows, width), F32), jax.ShapeDtypeStruct((1,), F32)],
-            in_specs=[vmem, vmem, smem],
+            in_specs=[hbm, hbm, smem],
             out_specs=[vmem, smem],
             scratch_shapes=[
+                pltpu.VMEM((rows, width), BF16),
+                pltpu.VMEM((rows // width, width), F32),
+                pltpu.SemaphoreType.DMA((2,)),
                 pltpu.VMEM((n_dev * n_tiles, width + AUG, TILE), BF16),
                 pltpu.VMEM((rows, 2 * width), BF16),
                 pltpu.VMEM((rows, width), F32),

time: 69.9 us -> 65.6 us (0.938)
  Pallas kernels: 64.2 us -> 60 us
    pallas_call x1, Pallas kernels: 64.2 us -> 60 us  [per_device(): pl.pallas_call(functools.partial(kernel, side, width), out_shape=[jax.Sha...]
where the time goes in v2:
time: 65.6 us; the launch traced here: 65.4 us
  Pallas kernels  60 us (91%)
  between operations  3.06 us (5%)
  local copies, waits for them, and re-layouts  2.43 us (4%)
    pallas_call x1, Pallas kernels, per_device(): pl.pallas_call(functools.partial(kernel, side, width), out_shape=[jax.Sha...  60 us
    unnamed x5, local copies, waits for them, and re-layouts  2.43 us

profile of v2, /device:TPU:97, one launch (start us, length us, event | category | flops | bytes accessed | tf_op | source)
XLA Modules:
  0.0 65.4 jit_solution(13741217160846787252)
XLA Ops:
  1.3 0.0 copy-start
  1.3 0.9 %copy-done = bf16[1024,128]{1,0:T(8,128)(2,1)S(1)} copy-done((bf16[1024,128]{1,0:T(8,128)(2,1)S(1)}, bf16[1024,128]{1,0:T(8,128)(2,1)}, u32[]{:S(2)}) %copy-start) | copy-done | bytes 262168
  2.2 0.0 copy-start.1
  2.2 0.7 %copy-done.1 = f32[1024]{0:T(1024)S(1)} copy-done((f32[1024]{0:T(1024)S(1)}, f32[1024]{0:T(1024)}, u32[]{:S(2)}) %copy-start.1) | copy-done | bytes 4120
  2.9 60.0 %pair_forces.1 = (f32[1024,128]{1,0:T(8,128)S(1)}, f32[1]{0:T(128)}) custom-call(bf16[1024,128]{1,0:T(8,128)(2,1)S(1)} %copy-done, f32[8,128]{1,0:T(8,128)S(1)} %bitcast.1, s32[1]{0:T(128)S(6)} %copy.7.cnt_ref), custom_call_target="tpu_custom_call" | custom-call | tf_op jit(solution)/shard_map/pair_forces/pallas_call | solution.py:292
  62.9 0.8 %copy.8 = f32[1024,128]{1,0:T(8,128)} copy(f32[1024,128]{1,0:T(8,128)S(1)} %get-tuple-element.4) | data formatting | bytes 1048576
Async XLA Ops:
  1.3 1.0 %copy-start = (bf16[1024,128]{1,0:T(8,128)(2,1)S(1)}, bf16[1024,128]{1,0:T(8,128)(2,1)}, u32[]{:S(2)}) copy-start(bf16[1024,128]{1,0:T(8,128)(2,1)} %x_hbm.1) | copy-start | bytes 786436
  2.2 0.7 %copy-start.1 = (f32[1024]{0:T(1024)S(1)}, f32[1024]{0:T(1024)}, u32[]{:S(2)}) copy-start(f32[1024]{0:T(1024)} %param.4) | copy-start | bytes 12292

commit v3 on v2

v3 whole, which is shorter than its diff:
```python
import functools
import math

import jax
import jax.numpy as jnp
from jax import lax
from jax.experimental import pallas as pl
from jax.experimental.pallas import tpu as pltpu
from jax.sharding import PartitionSpec as P

MESH = pl.DeviceIdType.MESH
BF16, F32 = jnp.bfloat16, jnp.float32
TILE = 256
AUG = 16
S_CAP = 1.69e38
C_CAP = 3.3895313892515355e38

SIDE, TILES = 4, 4
PAIRS = [(0, 2), (1, 1), (1, -1), (-1, 1), (-1, -1), (2, 0), (1, 2), (-1, 2), (2, 1), (2, -1), (2, 2)]
STAGES = [[((0, 1), t), ((0, -1), t), ((1, 0), t + 2), ((-1, 0), t + 2)] for t in (0, 1)]
STAGES += [[((1, 0), t), ((-1, 0), t), ((0, 1), t + 2), ((0, -1), t + 2)] for t in (0, 1)]
STAGES += [[((a, b), 0), ((a, b), 1), ((b, a), 2), ((b, a), 3)] for a, b in PAIRS]
STAGE_OF = {piece: (k, j) for k, stage in enumerate(STAGES) for j, piece in enumerate(stage)}
SHARE = (0.5, 0.5, 0.5, 0.5, 0.5, 1.0, 0.5, 0.5, 0.0, 0.5, 1.0, 0.0, 1.0, 0.0, 0.5)
COMPUTE = (0, 1, 2, 3, 4, 5, 6, 7, 10, 9, 12, 14, 8, 11, 13)
ARRIVALS = {0: (1,), 1: (2,), 2: (3,), 3: (4,), 4: (5, 6), 5: (7, 8), 6: (10, 11), 7: (9,), 8: (12,), 9: (14, 13)}
ENERGY_AT = 12


def wrap(d):
    return (d + 1) % SIDE - 1


def relays(piece):
    (slow, fast), t = piece
    swap = t >= TILES // 2
    if swap:
        slow, fast = fast, slow
    lead = 1 if t % 2 == 0 else -1
    hops = []
    if slow == 0 and fast == 0:
        hops += [(0, 1), (0, -1)]
    elif slow == 0 and fast == lead:
        hops += [(0, -fast)]
    if slow == 0:
        hops += [(1, 0), (-1, 0)]
    elif slow == lead:
        hops += [(-slow, 0)]
    return [(b, a) if swap else (a, b) for a, b in hops]


def relay_list(k):
    pieces = [((0, 0), t) for t in range(TILES)] if k < 0 else STAGES[k]
    found = []
    for piece in pieces:
        swap = piece[1] >= TILES // 2
        for hop in relays(piece):
            along = hop[1] if not swap else hop[0]
            found.append((0 if along else 1, len(found), piece, hop))
    return [(piece, hop) for _, _, piece, hop in sorted(found)]


def dot(lhs, rhs, dims):
    return lax.dot_general(lhs, rhs, (dims, ((), ())), preferred_element_type=F32)


def split3(val):
    hi = jnp.clip(val, -C_CAP, C_CAP).astype(BF16).astype(F32)
    mid = (val - hi).astype(BF16).astype(F32)
    low = (val - hi - mid).astype(BF16).astype(F32)
    return hi, mid, low


def kernel(width, x_hbm, q_hbm, cnt_ref, out_ref, e_ref, x_ref, q_ref, in_sem, slots, xa, ci, s_acc, t_acc, ebuf,
           send_sem, recv_sem, dsend_sem, drecv_sem, esend_sem, erecv_sem):
    rows = x_ref.shape[0]
    n_dev = 2 * SIDE * SIDE
    n_steps = len(STAGES)
    me = lax.axis_index('row')
    sys_id = lax.axis_index('sys')
    core = lax.rem(me, 2)
    chip = lax.div(me, 2)
    pos_y, pos_x = lax.div(chip, SIDE), lax.rem(chip, SIDE)
    mate = me + 1 - 2 * core
    scale = math.log2(math.e) / width

    def dev(dy, dx, plane):
        return (lax.rem(pos_y + dy + SIDE, SIDE) * SIDE + lax.rem(pos_x + dx + SIDE, SIDE)) * 2 + plane

    x_in = pltpu.make_async_copy(x_hbm, x_ref, in_sem.at[0])
    q_in = pltpu.make_async_copy(q_hbm, q_ref, in_sem.at[1])
    x_in.start()
    q_in.start()
    barrier = pltpu.get_barrier_semaphore()
    near = [dev(0, 1, core), dev(0, -1, core), dev(1, 0, core), dev(-1, 0, core), mate]
    for peer in near:
        pl.semaphore_signal(barrier, inc=1, device_id=(sys_id, peer), device_id_type=MESH)
    s_acc[...] = jnp.zeros_like(s_acc)
    t_acc[...] = jnp.zeros_like(t_acc)
    x_in.wait()
    q_in.wait()

    count = cnt_ref[0]
    row_id = lax.broadcasted_iota(jnp.int32, (rows, width), 0)
    lane_id = lax.broadcasted_iota(jnp.int32, (rows, width), 1)
    x_val = jnp.where(row_id < count, x_ref[...].astype(F32), 0.0)
    x_t = x_val.T
    s_row = -jnp.minimum(0.5 * jnp.sum(x_t * x_t, axis=0, keepdims=True), S_CAP)
    q_shape = q_ref.shape
    q_id = lax.broadcasted_iota(jnp.int32, q_shape, 0) * q_shape[1] + lax.broadcasted_iota(jnp.int32, q_shape, 1)
    q_val = jnp.where(q_id < count, q_ref[...], 0.0)
    q_row = jnp.concatenate([q_val[r:r + 1, :] for r in range(q_shape[0])], axis=1)
    aug_id = lax.broadcasted_iota(jnp.int32, (AUG, rows), 0)
    aug = jnp.where(aug_id < 3, 1.0, 0.0)
    for k, part in enumerate(split3(s_row) + split3(q_row)):
        aug = jnp.where(aug_id == 3 + k, part, aug)
    for t in range(TILES):
        cols = slice(t * TILE, (t + 1) * TILE)
        slots[me * TILES + t, :width, :] = x_t[:, cols].astype(BF16)
        slots[me * TILES + t, width:, :] = aug[:, cols].astype(BF16)
    pl.semaphore_wait(barrier, len(near))

    sends = []

    def unit_of(piece, plane):
        return dev(piece[0][0], piece[0][1], plane) * TILES + piece[1]

    def remote(unit, send, recv, peer):
        return pltpu.make_async_remote_copy(src_ref=slots.at[unit], dst_ref=slots.at[unit], send_sem=send, recv_sem=recv,
                                            device_id=(sys_id, peer), device_id_type=MESH)

    def start_relays(k):
        for piece, hop in relay_list(k):
            there = ((wrap(piece[0][0] - hop[0]), wrap(piece[0][1] - hop[1])), piece[1])
            remote(unit_of(piece, core), send_sem.at[len(sends)], recv_sem.at[STAGE_OF[there]],
                   dev(hop[0], hop[1], core)).start()
            sends.append(k)

    def pieces(k):
        return [((0, 0), t) for t in range(TILES)] if k < 0 else STAGES[k]

    def to_mate(k, j, plane):
        return remote(unit_of(pieces(k)[j], plane), dsend_sem.at[k + 1, j], drecv_sem.at[k + 1, j], mate)

    def arrive(k):
        for j in range(TILES):
            remote(unit_of(STAGES[k][j], core), send_sem.at[0], recv_sem.at[k, j], mate).wait_recv()
        start_relays(k)
        for j in range(TILES):
            to_mate(k, j, core).start()

    def from_mate(k):
        for j in range(TILES):
            to_mate(k, j, 1 - core).wait_recv()

    start_relays(-1)
    for j in range(TILES):
        to_mate(-1, j, core).start()

    s_col = -jnp.minimum(0.5 * jnp.sum(x_val * x_val, axis=1, keepdims=True), S_CAP)
    xa[:, :width] = x_val.astype(BF16)
    tail = jnp.where((lane_id >= 3) & (lane_id < 6), 1.0, 0.0)
    for k, part in enumerate(split3(s_col)):
        tail = jnp.where(lane_id == k, part, tail)
    xa[:, width:] = tail.astype(BF16)
    q_t = q_val.T
    for r in range(q_shape[0]):
        lanes = q_shape[1]
        ci[r * lanes:(r + 1) * lanes, :] = jnp.broadcast_to(q_t[:, r:r + 1], (lanes, width))

    eye = (lax.broadcasted_iota(jnp.int32, (TILE, TILE), 0) == lax.broadcasted_iota(jnp.int32, (TILE, TILE), 1))
    pad = jnp.zeros((width - AUG, TILE), BF16)

    def column_tile(unit, diag=None):
        block = slots[unit]
        rhs = jnp.concatenate([block, pad], axis=0)
        parts = block[width:, :].astype(F32)
        c_cols = parts[6:7, :] + parts[7:8, :] + parts[8:9, :]
        for it in range(rows // TILE):
            mine = slice(it * TILE, (it + 1) * TILE)
            arg = dot(xa[mine, :], rhs, ((1,), (0,)))
            weight = jnp.exp2(jnp.minimum(arg, 0.0) * scale) * c_cols
            if it == diag:
                weight = jnp.where(eye, 0.0, weight)
            c_mine = ci[mine, :]
            left, right = weight[:, :width] * c_mine, weight[:, width:] * c_mine
            s_acc[mine, :] += left + right
            w_low = jnp.concatenate([left, right], axis=1).astype(BF16)
            t_acc[mine, :] += dot(w_low, block[:width, :], ((1,), (1,)))

    for t in range(TILES):
        column_tile(me * TILES + t, diag=t)
    arrive(0)
    from_mate(-1)
    for t in range(TILES):
        column_tile(mate * TILES + t)
    ebuf[me] = jnp.zeros(ebuf.shape[1:], F32)

    def e_copy(step):
        return pltpu.make_async_remote_copy(
            src_ref=ebuf.at[me], dst_ref=ebuf.at[me], send_sem=esend_sem.at[step], recv_sem=erecv_sem.at[me],
            device_id=(sys_id, lax.rem(me + step, n_dev)), device_id_type=MESH)

    def e_start(step, carry):
        e_copy(step).start()
        return carry

    def tally(weight):
        ebuf[me] += weight * jnp.sum(s_acc[...].reshape(rows // 8, 8, width), axis=0)

    share = [0.5] + [SHARE[k] for k in COMPUTE]

    def step_units(step):
        units = []
        for j in range(TILES):
            code = jnp.int32(0)
            for now, k in enumerate(COMPUTE):
                (dy, dx), t = STAGES[k][j]
                code = jnp.where(step == now, ((dy % SIDE) * SIDE + dx % SIDE) * TILES + t, code)
            for plane in (core, 1 - core):
                units.append(dev(lax.div(code, SIDE * TILES), lax.rem(lax.div(code, TILES), SIDE), plane) * TILES
                             + lax.rem(code, TILES))
        return units

    def step_body(step, carry):
        for now in range(n_steps):
            @pl.when(step == now)
            def _():
                for k in ARRIVALS.get(now, ()):
                    arrive(k)
                from_mate(COMPUTE[now])
                if now <= ENERGY_AT and share[now] != share[now + 1]:
                    tally(share[now] - share[now + 1])
                if now == ENERGY_AT:
                    lax.fori_loop(1, n_dev, e_start, 0)
        for unit in step_units(step):
            column_tile(unit)
        return carry
    lax.fori_loop(0, n_steps, step_body, 0)

    s_sum = jnp.sum(s_acc[...], axis=1, keepdims=True)
    out_ref[...] = (s_sum * xa[:, :width].astype(F32) - t_acc[...]) * (1.0 / width)

    def e_wait(step, carry):
        src = lax.rem(me + step, n_dev)
        pltpu.make_async_remote_copy(
            src_ref=ebuf.at[src], dst_ref=ebuf.at[src], send_sem=esend_sem.at[step], recv_sem=erecv_sem.at[src],
            device_id=(sys_id, mate), device_id_type=MESH).wait_recv()
        return carry
    lax.fori_loop(1, n_dev, e_wait, 0)
    e_ref[0] = jnp.sum(ebuf[...])

    def e_sent(step, carry):
        e_copy(step).wait_send()
        return carry
    lax.fori_loop(1, n_dev, e_sent, 0)

    def sent(idx, carry):
        remote(0, send_sem.at[idx], recv_sem.at[0, 0], mate).wait_send()
        return carry
    lax.fori_loop(0, len(sends), sent, 0)

    def mate_sent(idx, carry):
        remote(0, dsend_sem.at[lax.div(idx, TILES), lax.rem(idx, TILES)], drecv_sem.at[0, 0], mate).wait_send()
        return carry
    lax.fori_loop(0, TILES * (len(STAGES) + 1), mate_sent, 0)


def solution(mesh):
    n_dev = mesh.shape['row']
    assert n_dev == 2 * SIDE * SIDE

    def per_device(positions, charges, counts):
        rows, width = positions.shape
        assert rows == TILE * TILES and 2 * width == TILE
        n_sends = sum(len(relay_list(k)) for k in range(-1, len(STAGES)))
        hbm = pl.BlockSpec(memory_space=pltpu.HBM)
        smem = pl.BlockSpec(memory_space=pltpu.SMEM)
        force, energy = pl.pallas_call(
            functools.partial(kernel, width),
            out_shape=[jax.ShapeDtypeStruct((rows, width), F32), jax.ShapeDtypeStruct((1,), F32)],
            in_specs=[hbm, hbm, smem],
            out_specs=[pl.BlockSpec(memory_space=pltpu.VMEM), smem],
            scratch_shapes=[
                pltpu.VMEM((rows, width), BF16),
                pltpu.VMEM((rows // width, width), F32),
                pltpu.SemaphoreType.DMA((2,)),
                pltpu.VMEM((n_dev * TILES, width + AUG, TILE), BF16),
                pltpu.VMEM((rows, 2 * width), BF16),
                pltpu.VMEM((rows, width), F32),
                pltpu.VMEM((rows, width), F32),
                pltpu.VMEM((rows, width), F32),
                pltpu.VMEM((n_dev, 8, width), F32),
                pltpu.SemaphoreType.DMA((n_sends,)),
                pltpu.SemaphoreType.DMA((len(STAGES), TILES)),
                pltpu.SemaphoreType.DMA((len(STAGES) + 1, TILES)),
                pltpu.SemaphoreType.DMA((len(STAGES) + 1, TILES)),
                pltpu.SemaphoreType.DMA((n_dev,)),
                pltpu.SemaphoreType.DMA((n_dev,)),
            ],
            compiler_params=pltpu.CompilerParams(collective_id=0, has_side_effects=True),
            name='pair_forces',
        )(positions, charges.reshape(rows // width, width), counts)
        return force, energy

    row_spec = P(('sys', 'row'), None)
    vec_spec = P(('sys', 'row'))
    return jax.shard_map(per_device, mesh=mesh, in_specs=(row_spec, vec_spec, vec_spec),
                         out_specs=(row_spec, P('sys')), check_vma=False)
```

time: 65.6 us -> 65.9 us (level)
  Pallas kernels: 60 us -> 60.9 us
    pallas_call x1, Pallas kernels: 60 us -> 60.9 us  [per_device(): pl.pallas_call(functools.partial(kernel, width), out_shape=[jax.ShapeDtyp...]
    unnamed x5 -> x1, local copies, waits for them, and re-layouts: 2.43 us -> 1.87 us
where the time goes in v3:
time: 65.9 us; the launch traced here: 65.7 us
  Pallas kernels  60.9 us (92%)
  between operations  2.98 us (5%)
  local copies, waits for them, and re-layouts  1.87 us (3%)
    pallas_call x1, Pallas kernels, per_device(): pl.pallas_call(functools.partial(kernel, width), out_shape=[jax.ShapeDtyp...  60.9 us
    unnamed x1, local copies, waits for them, and re-layouts  1.87 us

profile of v3, /device:TPU:97, one launch (start us, length us, event | category | flops | bytes accessed | tf_op | source)
XLA Modules:
  0.0 65.7 jit_solution(4437204656028735133)
XLA Ops:
  1.3 60.9 %pair_forces.1 = (f32[1024,128]{1,0:T(8,128)}, f32[1]{0:T(128)}) custom-call(bf16[1024,128]{1,0:T(8,128)(2,1)} %x_hbm.1, f32[8,128]{1,0:T(8,128)} %bitcast.1, s32[1]{0:T(128)S(6)} %copy.7.cnt_ref), custom_call_target="tpu_custom_call" | custom-call | tf_op jit(solution)/shard_map/pair_forces/pallas_call | solution.py:279
  62.1 1.9 %copy.8 = f32[1024,128]{1,0:T(8,128)} copy(f32[1024,128]{1,0:T(8,128)} %get-tuple-element.4) | data formatting | bytes 1048576

commit v4 on v3

--- a/solution.py
+++ b/solution.py
@@ -20,7 +20,7 @@
 STAGES = [[((0, 1), t), ((0, -1), t), ((1, 0), t + 2), ((-1, 0), t + 2)] for t in (0, 1)]
 STAGES += [[((1, 0), t), ((-1, 0), t), ((0, 1), t + 2), ((0, -1), t + 2)] for t in (0, 1)]
 STAGES += [[((a, b), 0), ((a, b), 1), ((b, a), 2), ((b, a), 3)] for a, b in PAIRS]
-STAGE_OF = {piece: (k, j) for k, stage in enumerate(STAGES) for j, piece in enumerate(stage)}
+STAGE_OF = {piece: k for k, stage in enumerate(STAGES) for piece in stage}
 SHARE = (0.5, 0.5, 0.5, 0.5, 0.5, 1.0, 0.5, 0.5, 0.0, 0.5, 1.0, 0.0, 1.0, 0.0, 0.5)
 COMPUTE = (0, 1, 2, 3, 4, 5, 6, 7, 10, 9, 12, 14, 8, 11, 13)
 ARRIVALS = {0: (1,), 1: (2,), 2: (3,), 3: (4,), 4: (5, 6), 5: (7, 8), 6: (10, 11), 7: (9,), 8: (12,), 9: (14, 13)}
@@ -60,6 +60,17 @@
     return [(piece, hop) for _, _, piece, hop in sorted(found)]
 
 
+def merged(copies, join):
+    found = []
+    for piece, hop in copies:
+        left = (piece[0], piece[1] - 1)
+        if join and piece[1] % 2 == 1 and (left, 1, hop) in found:
+            found[found.index((left, 1, hop))] = (left, 2, hop)
+        else:
+            found.append((piece, 1, hop))
+    return found
+
+
 def dot(lhs, rhs, dims):
     return lax.dot_general(lhs, rhs, (dims, ((), ())), preferred_element_type=F32)
 
@@ -72,10 +83,11 @@
 
 
 def kernel(width, x_hbm, q_hbm, cnt_ref, out_ref, e_ref, x_ref, q_ref, in_sem, slots, xa, ci, s_acc, t_acc, ebuf,
-           send_sem, recv_sem, dsend_sem, drecv_sem, esend_sem, erecv_sem):
+           send_sem, recv_sem, mate_sem, e_sem):
     rows = x_ref.shape[0]
     n_dev = 2 * SIDE * SIDE
     n_steps = len(STAGES)
+    n_sends = sum(len(relay_list(k)) for k in range(-1, len(STAGES)))
     me = lax.axis_index('row')
     sys_id = lax.axis_index('sys')
     core = lax.rem(me, 2)
@@ -120,42 +132,38 @@
         slots[me * TILES + t, width:, :] = aug[:, cols].astype(BF16)
     pl.semaphore_wait(barrier, len(near))
 
-    sends = []
-
     def unit_of(piece, plane):
         return dev(piece[0][0], piece[0][1], plane) * TILES + piece[1]
 
-    def remote(unit, send, recv, peer):
-        return pltpu.make_async_remote_copy(src_ref=slots.at[unit], dst_ref=slots.at[unit], send_sem=send, recv_sem=recv,
+    def remote(unit, tiles, send, recv, peer):
+        ref = slots.at[pl.ds(unit, tiles)]
+        return pltpu.make_async_remote_copy(src_ref=ref, dst_ref=ref, send_sem=send, recv_sem=recv,
                                             device_id=(sys_id, peer), device_id_type=MESH)
 
     def start_relays(k):
-        for piece, hop in relay_list(k):
+        for piece, tiles, hop in merged(relay_list(k), k >= 0):
             there = ((wrap(piece[0][0] - hop[0]), wrap(piece[0][1] - hop[1])), piece[1])
-            remote(unit_of(piece, core), send_sem.at[len(sends)], recv_sem.at[STAGE_OF[there]],
+            remote(unit_of(piece, core), tiles, send_sem.at[0], recv_sem.at[STAGE_OF[there]],
                    dev(hop[0], hop[1], core)).start()
-            sends.append(k)
-
-    def pieces(k):
-        return [((0, 0), t) for t in range(TILES)] if k < 0 else STAGES[k]
-
-    def to_mate(k, j, plane):
-        return remote(unit_of(pieces(k)[j], plane), dsend_sem.at[k + 1, j], drecv_sem.at[k + 1, j], mate)
+
+    def to_mate(k):
+        if k < 0:
+            groups = [(((0, 0), 0), TILES, None)]
+        else:
+            groups = merged([(piece, None) for piece in STAGES[k]], True)
+        for piece, tiles, _ in groups:
+            remote(unit_of(piece, core), tiles, send_sem.at[1], mate_sem.at[k + 1], mate).start()
 
     def arrive(k):
-        for j in range(TILES):
-            remote(unit_of(STAGES[k][j], core), send_sem.at[0], recv_sem.at[k, j], mate).wait_recv()
+        remote(0, TILES, send_sem.at[0], recv_sem.at[k], mate).wait_recv()
         start_relays(k)
-        for j in range(TILES):
-            to_mate(k, j, core).start()
+        to_mate(k)
 
     def from_mate(k):
-        for j in range(TILES):
-            to_mate(k, j, 1 - core).wait_recv()
+        remote(0, TILES, send_sem.at[1], mate_sem.at[k + 1], mate).wait_recv()
 
     start_relays(-1)
-    for j in range(TILES):
-        to_mate(-1, j, core).start()
+    to_mate(-1)
 
     s_col = -jnp.minimum(0.5 * jnp.sum(x_val * x_val, axis=1, keepdims=True), S_CAP)
     xa[:, :width] = x_val.astype(BF16)
@@ -196,13 +204,13 @@
         column_tile(mate * TILES + t)
     ebuf[me] = jnp.zeros(ebuf.shape[1:], F32)
 
-    def e_copy(step):
-        return pltpu.make_async_remote_copy(
-            src_ref=ebuf.at[me], dst_ref=ebuf.at[me], send_sem=esend_sem.at[step], recv_sem=erecv_sem.at[me],
-            device_id=(sys_id, lax.rem(me + step, n_dev)), device_id_type=MESH)
+    def e_copy(first, count, peer):
+        ref = ebuf.at[pl.ds(first, count)]
+        return pltpu.make_async_remote_copy(src_ref=ref, dst_ref=ref, send_sem=e_sem.at[0], recv_sem=e_sem.at[1],
+                                            device_id=(sys_id, peer), device_id_type=MESH)
 
     def e_start(step, carry):
-        e_copy(step).start()
+        e_copy(me, 1, lax.rem(me + step, n_dev)).start()
         return carry
 
     def tally(weight):
@@ -241,29 +249,11 @@
     s_sum = jnp.sum(s_acc[...], axis=1, keepdims=True)
     out_ref[...] = (s_sum * xa[:, :width].astype(F32) - t_acc[...]) * (1.0 / width)
 
-    def e_wait(step, carry):
-        src = lax.rem(me + step, n_dev)
-        pltpu.make_async_remote_copy(
-            src_ref=ebuf.at[src], dst_ref=ebuf.at[src], send_sem=esend_sem.at[step], recv_sem=erecv_sem.at[src],
-            device_id=(sys_id, mate), device_id_type=MESH).wait_recv()
-        return carry
-    lax.fori_loop(1, n_dev, e_wait, 0)
+    e_copy(0, n_dev - 1, mate).wait_recv()
     e_ref[0] = jnp.sum(ebuf[...])
-
-    def e_sent(step, carry):
-        e_copy(step).wait_send()
-        return carry
-    lax.fori_loop(1, n_dev, e_sent, 0)
-
-    def sent(idx, carry):
-        remote(0, send_sem.at[idx], recv_sem.at[0, 0], mate).wait_send()
-        return carry
-    lax.fori_loop(0, len(sends), sent, 0)
-
-    def mate_sent(idx, carry):
-        remote(0, dsend_sem.at[lax.div(idx, TILES), lax.rem(idx, TILES)], drecv_sem.at[0, 0], mate).wait_send()
-        return carry
-    lax.fori_loop(0, TILES * (len(STAGES) + 1), mate_sent, 0)
+    e_copy(0, n_dev - 1, mate).wait_send()
+    remote(0, n_sends, send_sem.at[0], recv_sem.at[0], mate).wait_send()
+    remote(0, TILES * (len(STAGES) + 1), send_sem.at[1], mate_sem.at[0], mate).wait_send()
 
 
 def solution(mesh):
@@ -273,7 +263,6 @@
     def per_device(positions, charges, counts):
         rows, width = positions.shape
         assert rows == TILE * TILES and 2 * width == TILE
-        n_sends = sum(len(relay_list(k)) for k in range(-1, len(STAGES)))
         hbm = pl.BlockSpec(memory_space=pltpu.HBM)
         smem = pl.BlockSpec(memory_space=pltpu.SMEM)
         force, energy = pl.pallas_call(
@@ -291,12 +280,10 @@
                 pltpu.VMEM((rows, width), F32),
                 pltpu.VMEM((rows, width), F32),
                 pltpu.VMEM((n_dev, 8, width), F32),
-                pltpu.SemaphoreType.DMA((n_sends,)),
-                pltpu.SemaphoreType.DMA((len(STAGES), TILES)),
-                pltpu.SemaphoreType.DMA((len(STAGES) + 1, TILES)),
-                pltpu.SemaphoreType.DMA((len(STAGES) + 1, TILES)),
-                pltpu.SemaphoreType.DMA((n_dev,)),
-                pltpu.SemaphoreType.DMA((n_dev,)),
+                pltpu.SemaphoreType.DMA((2,)),
+                pltpu.SemaphoreType.DMA((len(STAGES),)),
+                pltpu.SemaphoreType.DMA((len(STAGES) + 1,)),
+                pltpu.SemaphoreType.DMA((2,)),
             ],
             compiler_params=pltpu.CompilerParams(collective_id=0, has_side_effects=True),
             name='pair_forces',

time: 65.9 us -> 61.2 us (0.929)
  Pallas kernels: 60.9 us -> 56.2 us
    pallas_call x1, Pallas kernels: 60.9 us -> 56.2 us  [per_device(): pl.pallas_call(functools.partial(kernel, width), out_shape=[jax.ShapeDtyp...]
where the time goes in v4:
time: 61.2 us; the launch traced here: 61.1 us
  Pallas kernels  56.2 us (92%)
  between operations  2.98 us (5%)
  local copies, waits for them, and re-layouts  1.87 us (3%)
    pallas_call x1, Pallas kernels, per_device(): pl.pallas_call(functools.partial(kernel, width), out_shape=[jax.ShapeDtyp...  56.2 us
    unnamed x1, local copies, waits for them, and re-layouts  1.87 us

profile of v4, /device:TPU:97, one launch (start us, length us, event | category | flops | bytes accessed | tf_op | source)
XLA Modules:
  0.0 61.1 jit_solution(9349179070054871257)
XLA Ops:
  1.3 56.2 %pair_forces.1 = (f32[1024,128]{1,0:T(8,128)}, f32[1]{0:T(128)}) custom-call(bf16[1024,128]{1,0:T(8,128)(2,1)} %x_hbm.1, f32[8,128]{1,0:T(8,128)} %bitcast.1, s32[1]{0:T(128)S(6)} %copy.7.cnt_ref), custom_call_target="tpu_custom_call" | custom-call | tf_op jit(solution)/shard_map/pair_forces/pallas_call | solution.py:268
  57.5 1.9 %copy.8 = f32[1024,128]{1,0:T(8,128)} copy(f32[1024,128]{1,0:T(8,128)} %get-tuple-element.4) | data formatting | bytes 1048576

commit v5 on v4

--- a/solution.py
+++ b/solution.py
@@ -22,9 +22,10 @@
 STAGES += [[((a, b), 0), ((a, b), 1), ((b, a), 2), ((b, a), 3)] for a, b in PAIRS]
 STAGE_OF = {piece: k for k, stage in enumerate(STAGES) for piece in stage}
 SHARE = (0.5, 0.5, 0.5, 0.5, 0.5, 1.0, 0.5, 0.5, 0.0, 0.5, 1.0, 0.0, 1.0, 0.0, 0.5)
-COMPUTE = (0, 1, 2, 3, 4, 5, 6, 7, 10, 9, 12, 14, 8, 11, 13)
-ARRIVALS = {0: (1,), 1: (2,), 2: (3,), 3: (4,), 4: (5, 6), 5: (7, 8), 6: (10, 11), 7: (9,), 8: (12,), 9: (14, 13)}
-ENERGY_AT = 12
+LOOPS = [
+    [((1,), (0,)), ((2,), (1,)), ((3,), (2,)), ((4,), (3,)), ((5, 6), (4,)), ((7, 8), (5,)), ((), (8,))],
+    [((10, 11, 9, 12), (6, 7)), ((14, 13), (10, 12)), ((), (9, 14)), ((), (11, 13))],
+]
 
 
 def wrap(d):
@@ -86,7 +87,6 @@
            send_sem, recv_sem, mate_sem, e_sem):
     rows = x_ref.shape[0]
     n_dev = 2 * SIDE * SIDE
-    n_steps = len(STAGES)
     n_sends = sum(len(relay_list(k)) for k in range(-1, len(STAGES)))
     me = lax.axis_index('row')
     sys_id = lax.axis_index('sys')
@@ -216,35 +216,45 @@
     def tally(weight):
         ebuf[me] += weight * jnp.sum(s_acc[...].reshape(rows // 8, 8, width), axis=0)
 
-    share = [0.5] + [SHARE[k] for k in COMPUTE]
-
-    def step_units(step):
+    def step_units(steps, step, i):
         units = []
         for j in range(TILES):
             code = jnp.int32(0)
-            for now, k in enumerate(COMPUTE):
-                (dy, dx), t = STAGES[k][j]
+            for now, (_, computed) in enumerate(steps):
+                (dy, dx), t = STAGES[computed[i]][j]
                 code = jnp.where(step == now, ((dy % SIDE) * SIDE + dx % SIDE) * TILES + t, code)
             for plane in (core, 1 - core):
                 units.append(dev(lax.div(code, SIDE * TILES), lax.rem(lax.div(code, TILES), SIDE), plane) * TILES
                              + lax.rem(code, TILES))
         return units
 
-    def step_body(step, carry):
-        for now in range(n_steps):
-            @pl.when(step == now)
-            def _():
-                for k in ARRIVALS.get(now, ()):
-                    arrive(k)
-                from_mate(COMPUTE[now])
-                if now <= ENERGY_AT and share[now] != share[now + 1]:
-                    tally(share[now] - share[now + 1])
-                if now == ENERGY_AT:
-                    lax.fori_loop(1, n_dev, e_start, 0)
-        for unit in step_units(step):
-            column_tile(unit)
-        return carry
-    lax.fori_loop(0, n_steps, step_body, 0)
+    def run_loop(steps, share, share_after):
+        shares = [share] + [SHARE[computed[0]] for _, computed in steps]
+
+        def step_body(step, carry):
+            for now, (arriving, computed) in enumerate(steps):
+                @pl.when(step == now)
+                def _():
+                    for k in arriving:
+                        arrive(k)
+                    for k in computed:
+                        assert SHARE[k] == SHARE[computed[0]]
+                        from_mate(k)
+                    if shares[now] != shares[now + 1]:
+                        tally(shares[now] - shares[now + 1])
+                    if share_after is None and now == len(steps) - 1:
+                        assert SHARE[computed[0]] == 0.0
+                        lax.fori_loop(1, n_dev, e_start, 0)
+            for i in range(len(steps[0][1])):
+                for unit in step_units(steps, step, i):
+                    column_tile(unit)
+            return carry
+        lax.fori_loop(0, len(steps), step_body, 0)
+        return shares[-1]
+
+    last_share = 0.5
+    for n, steps in enumerate(LOOPS):
+        last_share = run_loop(steps, last_share, None if n == len(LOOPS) - 1 else 1)
 
     s_sum = jnp.sum(s_acc[...], axis=1, keepdims=True)
     out_ref[...] = (s_sum * xa[:, :width].astype(F32) - t_acc[...]) * (1.0 / width)

time: 61.2 us -> 58.9 us (0.962)
  Pallas kernels: 56.2 us -> 53.9 us
    pallas_call x1, Pallas kernels: 56.2 us -> 53.9 us  [per_device(): pl.pallas_call(functools.partial(kernel, width), out_shape=[jax.ShapeDtyp...]
where the time goes in v5:
time: 58.9 us; the launch traced here: 58.8 us
  Pallas kernels  53.9 us (92%)
  between operations  2.98 us (5%)
  local copies, waits for them, and re-layouts  1.87 us (3%)
    pallas_call x1, Pallas kernels, per_device(): pl.pallas_call(functools.partial(kernel, width), out_shape=[jax.ShapeDtyp...  53.9 us
    unnamed x1, local copies, waits for them, and re-layouts  1.87 us

profile of v5, /device:TPU:97, one launch (start us, length us, event | category | flops | bytes accessed | tf_op | source)
XLA Modules:
  0.0 58.8 jit_solution(15242356299172877091)
XLA Ops:
  1.3 53.9 %pair_forces.1 = (f32[1024,128]{1,0:T(8,128)}, f32[1]{0:T(128)}) custom-call(bf16[1024,128]{1,0:T(8,128)(2,1)} %x_hbm.1, f32[8,128]{1,0:T(8,128)} %bitcast.1, s32[1]{0:T(128)S(6)} %copy.7.cnt_ref), custom_call_target="tpu_custom_call" | custom-call | tf_op jit(solution)/shard_map/pair_forces/pallas_call | solution.py:278
  55.2 1.9 %copy.8 = f32[1024,128]{1,0:T(8,128)} copy(f32[1024,128]{1,0:T(8,128)} %get-tuple-element.4) | data formatting | bytes 1048576

commit v6 on v5

--- a/solution.py
+++ b/solution.py
@@ -16,15 +16,18 @@
 C_CAP = 3.3895313892515355e38
 
 SIDE, TILES = 4, 4
-PAIRS = [(0, 2), (1, 1), (1, -1), (-1, 1), (-1, -1), (2, 0), (1, 2), (-1, 2), (2, 1), (2, -1), (2, 2)]
+PAIRS = [(2, 0), (1, 2), (-1, 2), (2, 1), (2, -1), (2, 2)]
 STAGES = [[((0, 1), t), ((0, -1), t), ((1, 0), t + 2), ((-1, 0), t + 2)] for t in (0, 1)]
 STAGES += [[((1, 0), t), ((-1, 0), t), ((0, 1), t + 2), ((0, -1), t + 2)] for t in (0, 1)]
+CORNERS = [[((1, s), t), ((-1, s), t), ((s, 1), t + 2), ((s, -1), t + 2)] for t in (0, 1) for s in (1, -1)]
+STAGES += CORNERS[:2] + [[((0, 2), 0), ((0, 2), 1), ((2, 0), 2), ((2, 0), 3)]] + CORNERS[2:]
 STAGES += [[((a, b), 0), ((a, b), 1), ((b, a), 2), ((b, a), 3)] for a, b in PAIRS]
 STAGE_OF = {piece: k for k, stage in enumerate(STAGES) for piece in stage}
-SHARE = (0.5, 0.5, 0.5, 0.5, 0.5, 1.0, 0.5, 0.5, 0.0, 0.5, 1.0, 0.0, 1.0, 0.0, 0.5)
+SHARE = (0.5, 0.5, 0.5, 0.5, 0.5, 0.5, 0.5, 0.5, 0.5, 0.5, 1.0, 0.0, 1.0, 0.0, 0.5)
+RELAYS = {0: ((0, (0,)),), 1: ((1, (0,)), (0, (1,)), (1, (1,)))}
 LOOPS = [
-    [((1,), (0,)), ((2,), (1,)), ((3,), (2,)), ((4,), (3,)), ((5, 6), (4,)), ((7, 8), (5,)), ((), (8,))],
-    [((10, 11, 9, 12), (6, 7)), ((14, 13), (10, 12)), ((), (9, 14)), ((), (11, 13))],
+    [((1,), (0,)), ((2,), (1,)), ((3,), (2,)), ((6, 4), (3,)), ((5,), (6,))],
+    [((7, 8), (4, 5)), ((9, 10, 11), (7, 8)), ((12, 13, 14), (9, 10)), ((), (12, 14)), ((), (11, 13))],
 ]
 
 
@@ -50,7 +53,7 @@
     return [(b, a) if swap else (a, b) for a, b in hops]
 
 
-def relay_list(k):
+def relay_list(k, ranks=(0, 1)):
     pieces = [((0, 0), t) for t in range(TILES)] if k < 0 else STAGES[k]
     found = []
     for piece in pieces:
@@ -58,7 +61,7 @@
         for hop in relays(piece):
             along = hop[1] if not swap else hop[0]
             found.append((0 if along else 1, len(found), piece, hop))
-    return [(piece, hop) for _, _, piece, hop in sorted(found)]
+    return [(piece, hop) for rank, _, piece, hop in sorted(found) if rank in ranks]
 
 
 def merged(copies, join):
@@ -83,7 +86,7 @@
     return hi, mid, low
 
 
-def kernel(width, x_hbm, q_hbm, cnt_ref, out_ref, e_ref, x_ref, q_ref, in_sem, slots, xa, ci, s_acc, t_acc, ebuf,
+def kernel(width, x_hbm, q_hbm, cnt_ref, out_ref, e_ref, x_ref, q_ref, in_sem, slots, xa, ci, s_acc, t_acc, e_acc, ebuf,
            send_sem, recv_sem, mate_sem, e_sem):
     rows = x_ref.shape[0]
     n_dev = 2 * SIDE * SIDE
@@ -140,8 +143,8 @@
         return pltpu.make_async_remote_copy(src_ref=ref, dst_ref=ref, send_sem=send, recv_sem=recv,
                                             device_id=(sys_id, peer), device_id_type=MESH)
 
-    def start_relays(k):
-        for piece, tiles, hop in merged(relay_list(k), k >= 0):
+    def start_relays(k, ranks):
+        for piece, tiles, hop in merged(relay_list(k, ranks), k >= 0):
             there = ((wrap(piece[0][0] - hop[0]), wrap(piece[0][1] - hop[1])), piece[1])
             remote(unit_of(piece, core), tiles, send_sem.at[0], recv_sem.at[STAGE_OF[there]],
                    dev(hop[0], hop[1], core)).start()
@@ -156,13 +159,14 @@
 
     def arrive(k):
         remote(0, TILES, send_sem.at[0], recv_sem.at[k], mate).wait_recv()
-        start_relays(k)
+        for other, ranks in RELAYS.get(k, ((k, (0, 1)),)):
+            start_relays(other, ranks)
         to_mate(k)
 
     def from_mate(k):
         remote(0, TILES, send_sem.at[1], mate_sem.at[k + 1], mate).wait_recv()
 
-    start_relays(-1)
+    start_relays(-1, (0, 1))
     to_mate(-1)
 
     s_col = -jnp.minimum(0.5 * jnp.sum(x_val * x_val, axis=1, keepdims=True), S_CAP)
@@ -202,7 +206,7 @@
     from_mate(-1)
     for t in range(TILES):
         column_tile(mate * TILES + t)
-    ebuf[me] = jnp.zeros(ebuf.shape[1:], F32)
+    e_acc[...] = jnp.zeros_like(e_acc)
 
     def e_copy(first, count, peer):
         ref = ebuf.at[pl.ds(first, count)]
@@ -214,7 +218,7 @@
         return carry
 
     def tally(weight):
-        ebuf[me] += weight * jnp.sum(s_acc[...].reshape(rows // 8, 8, width), axis=0)
+        e_acc[...] += weight * jnp.sum(s_acc[...].reshape(rows // 8, 8, width), axis=0)
 
     def step_units(steps, step, i):
         units = []
@@ -229,7 +233,9 @@
         return units
 
     def run_loop(steps, share, share_after):
-        shares = [share] + [SHARE[computed[0]] for _, computed in steps]
+        shares = [share] + [SHARE[computed[-1]] for _, computed in steps]
+        starts = [SHARE[computed[0]] for _, computed in steps]
+        inner = [SHARE[computed[0]] - SHARE[computed[-1]] for _, computed in steps]
 
         def step_body(step, carry):
             for now, (arriving, computed) in enumerate(steps):
@@ -238,14 +244,19 @@
                     for k in arriving:
                         arrive(k)
                     for k in computed:
-                        assert SHARE[k] == SHARE[computed[0]]
                         from_mate(k)
-                    if shares[now] != shares[now + 1]:
-                        tally(shares[now] - shares[now + 1])
+                    if shares[now] != starts[now]:
+                        tally(shares[now] - starts[now])
                     if share_after is None and now == len(steps) - 1:
-                        assert SHARE[computed[0]] == 0.0
+                        assert not any(SHARE[k] for k in computed)
+                        ebuf[me] = e_acc[...]
                         lax.fori_loop(1, n_dev, e_start, 0)
             for i in range(len(steps[0][1])):
+                if i and any(inner):
+                    weight = jnp.float32(0.0)
+                    for now, change in enumerate(inner):
+                        weight = jnp.where(step == now, change, weight)
+                    tally(weight)
                 for unit in step_units(steps, step, i):
                     column_tile(unit)
             return carry
@@ -289,6 +300,7 @@
                 pltpu.VMEM((rows, width), F32),
                 pltpu.VMEM((rows, width), F32),
                 pltpu.VMEM((rows, width), F32),
+                pltpu.VMEM((8, width), F32),
                 pltpu.VMEM((n_dev, 8, width), F32),
                 pltpu.SemaphoreType.DMA((2,)),
                 pltpu.SemaphoreType.DMA((len(STAGES),)),

time: 58.9 us -> 58.1 us (0.986)
  Pallas kernels: 53.9 us -> 53.1 us
    pallas_call x1, Pallas kernels: 53.9 us -> 53.1 us  [per_device(): pl.pallas_call(functools.partial(kernel, width), out_shape=[jax.ShapeDtyp...]
where the time goes in v6:
time: 58.1 us; the launch traced here: 57.9 us
  Pallas kernels  53.1 us (91%)
  between operations  2.98 us (5%)
  local copies, waits for them, and re-layouts  1.87 us (3%)
    pallas_call x1, Pallas kernels, per_device(): pl.pallas_call(functools.partial(kernel, width), out_shape=[jax.ShapeDtyp...  53.1 us
    unnamed x1, local copies, waits for them, and re-layouts  1.87 us

profile of v6, /device:TPU:97, one launch (start us, length us, event | category | flops | bytes accessed | tf_op | source)
XLA Modules:
  0.0 57.9 jit_solution(15797334415339051159)
XLA Ops:
  1.3 53.1 %pair_forces.1 = (f32[1024,128]{1,0:T(8,128)}, f32[1]{0:T(128)}) custom-call(bf16[1024,128]{1,0:T(8,128)(2,1)} %x_hbm.1, f32[8,128]{1,0:T(8,128)} %bitcast.1, s32[1]{0:T(128)S(6)} %copy.7.cnt_ref), custom_call_target="tpu_custom_call" | custom-call | tf_op jit(solution)/shard_map/pair_forces/pallas_call | solution.py:289
  54.4 1.9 %copy.8 = f32[1024,128]{1,0:T(8,128)} copy(f32[1024,128]{1,0:T(8,128)} %get-tuple-element.4) | data formatting | bytes 1048576

commit v7 on v6

--- a/solution.py
+++ b/solution.py
@@ -22,13 +22,17 @@
 CORNERS = [[((1, s), t), ((-1, s), t), ((s, 1), t + 2), ((s, -1), t + 2)] for t in (0, 1) for s in (1, -1)]
 STAGES += CORNERS[:2] + [[((0, 2), 0), ((0, 2), 1), ((2, 0), 2), ((2, 0), 3)]] + CORNERS[2:]
 STAGES += [[((a, b), 0), ((a, b), 1), ((b, a), 2), ((b, a), 3)] for a, b in PAIRS]
-STAGE_OF = {piece: k for k, stage in enumerate(STAGES) for piece in stage}
+STAGE_OF = {piece: (k, j) for k, stage in enumerate(STAGES) for j, piece in enumerate(stage)}
+STAGE_OF.update({((0, 0), t): (-1, t) for t in range(TILES)})
 SHARE = (0.5, 0.5, 0.5, 0.5, 0.5, 0.5, 0.5, 0.5, 0.5, 0.5, 1.0, 0.0, 1.0, 0.0, 0.5)
 RELAYS = {0: ((0, (0,)),), 1: ((1, (0,)), (0, (1,)), (1, (1,)))}
 LOOPS = [
     [((1,), (0,)), ((2,), (1,)), ((3,), (2,)), ((6, 4), (3,)), ((5,), (6,))],
     [((7, 8), (4, 5)), ((9, 10, 11), (7, 8)), ((12, 13, 14), (9, 10)), ((), (12, 14)), ((), (11, 13))],
 ]
+
+
+PLACE = {k: n for n, k in enumerate([-1] + [k for steps in LOOPS for _, computed in steps for k in computed])}
 
 
 def wrap(d):
@@ -68,7 +72,8 @@
     found = []
     for piece, hop in copies:
         left = (piece[0], piece[1] - 1)
-        if join and piece[1] % 2 == 1 and (left, 1, hop) in found:
+        beside = join and piece[1] % 2 == 1 and STAGE_OF[left][0] == STAGE_OF[piece][0]
+        if beside and (left, 1, hop) in found:
             found[found.index((left, 1, hop))] = (left, 2, hop)
         else:
             found.append((piece, 1, hop))
@@ -131,40 +136,39 @@
         aug = jnp.where(aug_id == 3 + k, part, aug)
     for t in range(TILES):
         cols = slice(t * TILE, (t + 1) * TILE)
-        slots[me * TILES + t, :width, :] = x_t[:, cols].astype(BF16)
-        slots[me * TILES + t, width:, :] = aug[:, cols].astype(BF16)
+        slots[t, :width, :] = x_t[:, cols].astype(BF16)
+        slots[t, width:, :] = aug[:, cols].astype(BF16)
     pl.semaphore_wait(barrier, len(near))
 
-    def unit_of(piece, plane):
-        return dev(piece[0][0], piece[0][1], plane) * TILES + piece[1]
-
-    def remote(unit, tiles, send, recv, peer):
-        ref = slots.at[pl.ds(unit, tiles)]
-        return pltpu.make_async_remote_copy(src_ref=ref, dst_ref=ref, send_sem=send, recv_sem=recv,
-                                            device_id=(sys_id, peer), device_id_type=MESH)
+    other = n_dev // 2 * TILES
+
+    def unit_of(piece):
+        k, j = STAGE_OF[piece]
+        return PLACE[k] * TILES + j
+
+    def remote(src, dst, tiles, send, recv, peer):
+        return pltpu.make_async_remote_copy(
+            src_ref=slots.at[pl.ds(src, tiles)], dst_ref=slots.at[pl.ds(dst, tiles)], send_sem=send, recv_sem=recv,
+            device_id=(sys_id, peer), device_id_type=MESH)
 
     def start_relays(k, ranks):
         for piece, tiles, hop in merged(relay_list(k, ranks), k >= 0):
             there = ((wrap(piece[0][0] - hop[0]), wrap(piece[0][1] - hop[1])), piece[1])
-            remote(unit_of(piece, core), tiles, send_sem.at[0], recv_sem.at[STAGE_OF[there]],
+            remote(unit_of(piece), unit_of(there), tiles, send_sem.at[0], recv_sem.at[STAGE_OF[there][0]],
                    dev(hop[0], hop[1], core)).start()
 
     def to_mate(k):
-        if k < 0:
-            groups = [(((0, 0), 0), TILES, None)]
-        else:
-            groups = merged([(piece, None) for piece in STAGES[k]], True)
-        for piece, tiles, _ in groups:
-            remote(unit_of(piece, core), tiles, send_sem.at[1], mate_sem.at[k + 1], mate).start()
+        first = PLACE[k] * TILES
+        remote(first, other + first, TILES, send_sem.at[1], mate_sem.at[k + 1], mate).start()
 
     def arrive(k):
-        remote(0, TILES, send_sem.at[0], recv_sem.at[k], mate).wait_recv()
-        for other, ranks in RELAYS.get(k, ((k, (0, 1)),)):
-            start_relays(other, ranks)
+        remote(0, PLACE[k] * TILES, TILES, send_sem.at[0], recv_sem.at[k], mate).wait_recv()
+        for stage, ranks in RELAYS.get(k, ((k, (0, 1)),)):
+            start_relays(stage, ranks)
         to_mate(k)
 
     def from_mate(k):
-        remote(0, TILES, send_sem.at[1], mate_sem.at[k + 1], mate).wait_recv()
+        remote(0, other + PLACE[k] * TILES, TILES, send_sem.at[1], mate_sem.at[k + 1], mate).wait_recv()
 
     start_relays(-1, (0, 1))
     to_mate(-1)
@@ -201,11 +205,11 @@
             t_acc[mine, :] += dot(w_low, block[:width, :], ((1,), (1,)))
 
     for t in range(TILES):
-        column_tile(me * TILES + t, diag=t)
+        column_tile(t, diag=t)
     arrive(0)
     from_mate(-1)
     for t in range(TILES):
-        column_tile(mate * TILES + t)
+        column_tile(other + t)
     e_acc[...] = jnp.zeros_like(e_acc)
 
     def e_copy(first, count, peer):
@@ -219,18 +223,6 @@
 
     def tally(weight):
         e_acc[...] += weight * jnp.sum(s_acc[...].reshape(rows // 8, 8, width), axis=0)
-
-    def step_units(steps, step, i):
-        units = []
-        for j in range(TILES):
-            code = jnp.int32(0)
-            for now, (_, computed) in enumerate(steps):
-                (dy, dx), t = STAGES[computed[i]][j]
-                code = jnp.where(step == now, ((dy % SIDE) * SIDE + dx % SIDE) * TILES + t, code)
-            for plane in (core, 1 - core):
-                units.append(dev(lax.div(code, SIDE * TILES), lax.rem(lax.div(code, TILES), SIDE), plane) * TILES
-                             + lax.rem(code, TILES))
-        return units
 
     def run_loop(steps, share, share_after):
         shares = [share] + [SHARE[computed[-1]] for _, computed in steps]
@@ -257,8 +249,10 @@
                     for now, change in enumerate(inner):
                         weight = jnp.where(step == now, change, weight)
                     tally(weight)
-                for unit in step_units(steps, step, i):
-                    column_tile(unit)
+                first = (PLACE[steps[0][1][0]] + step * len(steps[0][1]) + i) * TILES
+                for j in range(TILES):
+                    column_tile(first + j)
+                    column_tile(other + first + j)
             return carry
         lax.fori_loop(0, len(steps), step_body, 0)
         return shares[-1]
@@ -273,8 +267,8 @@
     e_copy(0, n_dev - 1, mate).wait_recv()
     e_ref[0] = jnp.sum(ebuf[...])
     e_copy(0, n_dev - 1, mate).wait_send()
-    remote(0, n_sends, send_sem.at[0], recv_sem.at[0], mate).wait_send()
-    remote(0, TILES * (len(STAGES) + 1), send_sem.at[1], mate_sem.at[0], mate).wait_send()
+    remote(0, 0, n_sends, send_sem.at[0], recv_sem.at[0], mate).wait_send()
+    remote(0, 0, other, send_sem.at[1], mate_sem.at[0], mate).wait_send()
 
 
 def solution(mesh):

time: 58.1 us -> 57.6 us (level)
  Pallas kernels: 53.1 us -> 52.5 us
where the time goes in v7:
time: 57.6 us; the launch traced here: 57.4 us
  Pallas kernels  52.5 us (91%)
  between operations  2.98 us (5%)
  local copies, waits for them, and re-layouts  1.87 us (3%)
    pallas_call x1, Pallas kernels, per_device(): pl.pallas_call(functools.partial(kernel, width), out_shape=[jax.ShapeDtyp...  52.5 us
    unnamed x1, local copies, waits for them, and re-layouts  1.87 us

profile of v7, /device:TPU:97, one launch (start us, length us, event | category | flops | bytes accessed | tf_op | source)
XLA Modules:
  0.0 57.4 jit_solution(16798232181336647018)
XLA Ops:
  1.3 52.5 %pair_forces.1 = (f32[1024,128]{1,0:T(8,128)}, f32[1]{0:T(128)}) custom-call(bf16[1024,128]{1,0:T(8,128)(2,1)} %x_hbm.1, f32[8,128]{1,0:T(8,128)} %bitcast.1, s32[1]{0:T(128)S(6)} %copy.7.cnt_ref), custom_call_target="tpu_custom_call" | custom-call | tf_op jit(solution)/shard_map/pair_forces/pallas_call | solution.py:283
  53.8 1.9 %copy.8 = f32[1024,128]{1,0:T(8,128)} copy(f32[1024,128]{1,0:T(8,128)} %get-tuple-element.4) | data formatting | bytes 1048576

commit v8 on v7

--- a/solution.py
+++ b/solution.py
@@ -206,11 +206,34 @@
 
     for t in range(TILES):
         column_tile(t, diag=t)
-    arrive(0)
     from_mate(-1)
     for t in range(TILES):
         column_tile(other + t)
     e_acc[...] = jnp.zeros_like(e_acc)
+    arrive(0)
+    for t in range(TILES):
+        column_tile(TILES + t)
+
+    early = LOOPS[0]
+    assert all(SHARE[k] == 0.5 for _, computed in early for k in computed)
+
+    def early_body(step, carry):
+        for now, (arriving, computed) in enumerate(early[:-1]):
+            @pl.when(step == now)
+            def _():
+                for k in arriving:
+                    arrive(k)
+                from_mate(computed[0])
+        for j in range(TILES):
+            column_tile(other + (step + 1) * TILES + j)
+            column_tile((step + 2) * TILES + j)
+        return carry
+    lax.fori_loop(0, len(early) - 1, early_body, 0)
+    for k in early[-1][0]:
+        arrive(k)
+    from_mate(early[-1][1][0])
+    for j in range(TILES):
+        column_tile(other + len(early) * TILES + j)
 
     def e_copy(first, count, peer):
         ref = ebuf.at[pl.ds(first, count)]
@@ -257,9 +280,7 @@
         lax.fori_loop(0, len(steps), step_body, 0)
         return shares[-1]
 
-    last_share = 0.5
-    for n, steps in enumerate(LOOPS):
-        last_share = run_loop(steps, last_share, None if n == len(LOOPS) - 1 else 1)
+    run_loop(LOOPS[1], 0.5, None)
 
     s_sum = jnp.sum(s_acc[...], axis=1, keepdims=True)
     out_ref[...] = (s_sum * xa[:, :width].astype(F32) - t_acc[...]) * (1.0 / width)

time: 57.6 us -> 56.8 us (0.986)
  Pallas kernels: 52.5 us -> 51.8 us
    pallas_call x1, Pallas kernels: 52.5 us -> 51.8 us  [per_device(): pl.pallas_call(functools.partial(kernel, width), out_shape=[jax.ShapeDtyp...]
where the time goes in v8:
time: 56.8 us; the launch traced here: 56.6 us
  Pallas kernels  51.8 us (91%)
  between operations  2.98 us (5%)
  local copies, waits for them, and re-layouts  1.87 us (3%)
    pallas_call x1, Pallas kernels, per_device(): pl.pallas_call(functools.partial(kernel, width), out_shape=[jax.ShapeDtyp...  51.8 us
    unnamed x1, local copies, waits for them, and re-layouts  1.87 us

profile of v8, /device:TPU:97, one launch (start us, length us, event | category | flops | bytes accessed | tf_op | source)
XLA Modules:
  0.0 56.6 jit_solution(1341968325249462236)
XLA Ops:
  1.3 51.8 %pair_forces.1 = (f32[1024,128]{1,0:T(8,128)}, f32[1]{0:T(128)}) custom-call(bf16[1024,128]{1,0:T(8,128)(2,1)} %x_hbm.1, f32[8,128]{1,0:T(8,128)} %bitcast.1, s32[1]{0:T(128)S(6)} %copy.7.cnt_ref), custom_call_target="tpu_custom_call" | custom-call | tf_op jit(solution)/shard_map/pair_forces/pallas_call | solution.py:304
  53.1 1.9 %copy.8 = f32[1024,128]{1,0:T(8,128)} copy(f32[1024,128]{1,0:T(8,128)} %get-tuple-element.4) | data formatting | bytes 1048576

commit v9 on v8

--- a/solution.py
+++ b/solution.py
@@ -91,7 +91,7 @@
     return hi, mid, low
 
 
-def kernel(width, x_hbm, q_hbm, cnt_ref, out_ref, e_ref, x_ref, q_ref, in_sem, slots, xa, ci, s_acc, t_acc, e_acc, ebuf,
+def kernel(width, x_ref, q_ref, cnt_ref, out_ref, e_ref, slots, xa, ci, s_acc, t_acc, e_acc, ebuf,
            send_sem, recv_sem, mate_sem, e_sem):
     rows = x_ref.shape[0]
     n_dev = 2 * SIDE * SIDE
@@ -107,18 +107,12 @@
     def dev(dy, dx, plane):
         return (lax.rem(pos_y + dy + SIDE, SIDE) * SIDE + lax.rem(pos_x + dx + SIDE, SIDE)) * 2 + plane
 
-    x_in = pltpu.make_async_copy(x_hbm, x_ref, in_sem.at[0])
-    q_in = pltpu.make_async_copy(q_hbm, q_ref, in_sem.at[1])
-    x_in.start()
-    q_in.start()
     barrier = pltpu.get_barrier_semaphore()
     near = [dev(0, 1, core), dev(0, -1, core), dev(1, 0, core), dev(-1, 0, core), mate]
     for peer in near:
         pl.semaphore_signal(barrier, inc=1, device_id=(sys_id, peer), device_id_type=MESH)
     s_acc[...] = jnp.zeros_like(s_acc)
     t_acc[...] = jnp.zeros_like(t_acc)
-    x_in.wait()
-    q_in.wait()
 
     count = cnt_ref[0]
     row_id = lax.broadcasted_iota(jnp.int32, (rows, width), 0)
@@ -192,11 +186,12 @@
         rhs = jnp.concatenate([block, pad], axis=0)
         parts = block[width:, :].astype(F32)
         c_cols = parts[6:7, :] + parts[7:8, :] + parts[8:9, :]
-        for it in range(rows // TILE):
-            mine = slice(it * TILE, (it + 1) * TILE)
+        high = TILE if diag is not None else 2 * TILE
+        for it in range(rows // high):
+            mine = slice(it * high, (it + 1) * high)
             arg = dot(xa[mine, :], rhs, ((1,), (0,)))
             weight = jnp.exp2(jnp.minimum(arg, 0.0) * scale) * c_cols
-            if it == diag:
+            if diag is not None and it == diag:
                 weight = jnp.where(eye, 0.0, weight)
             c_mine = ci[mine, :]
             left, right = weight[:, :width] * c_mine, weight[:, width:] * c_mine
@@ -299,17 +294,14 @@
     def per_device(positions, charges, counts):
         rows, width = positions.shape
         assert rows == TILE * TILES and 2 * width == TILE
-        hbm = pl.BlockSpec(memory_space=pltpu.HBM)
+        vmem = pl.BlockSpec(memory_space=pltpu.VMEM)
         smem = pl.BlockSpec(memory_space=pltpu.SMEM)
         force, energy = pl.pallas_call(
             functools.partial(kernel, width),
             out_shape=[jax.ShapeDtypeStruct((rows, width), F32), jax.ShapeDtypeStruct((1,), F32)],
-            in_specs=[hbm, hbm, smem],
+            in_specs=[vmem, vmem, smem],
             out_specs=[pl.BlockSpec(memory_space=pltpu.VMEM), smem],
             scratch_shapes=[
-                pltpu.VMEM((rows, width), BF16),
-                pltpu.VMEM((rows // width, width), F32),
-                pltpu.SemaphoreType.DMA((2,)),
                 pltpu.VMEM((n_dev * TILES, width + AUG, TILE), BF16),
                 pltpu.VMEM((rows, 2 * width), BF16),
                 pltpu.VMEM((rows, width), F32),
@@ -322,7 +314,7 @@
                 pltpu.SemaphoreType.DMA((len(STAGES) + 1,)),
                 pltpu.SemaphoreType.DMA((2,)),
             ],
-            compiler_params=pltpu.CompilerParams(collective_id=0, has_side_effects=True),
+            compiler_params=pltpu.CompilerParams(collective_id=0, has_side_effects=True, vmem_limit_bytes=48 * 2 ** 20),
             name='pair_forces',
         )(positions, charges.reshape(rows // width, width), counts)
         return force, energy

time: 56.8 us -> 56.8 us (level)
  Pallas kernels: 51.8 us -> 51.1 us
    pallas_call x1, Pallas kernels: 51.8 us -> 51.1 us  [per_device(): pl.pallas_call(functools.partial(kernel, width), out_shape=[jax.ShapeDtyp...]
    unnamed x1 -> x5, local copies, waits for them, and re-layouts: 1.87 us -> 2.43 us
where the time goes in v9:
time: 56.8 us; the launch traced here: 56.6 us
  Pallas kernels  51.1 us (90%)
  between operations  3.06 us (5%)
  local copies, waits for them, and re-layouts  2.43 us (4%)
    pallas_call x1, Pallas kernels, per_device(): pl.pallas_call(functools.partial(kernel, width), out_shape=[jax.ShapeDtyp...  51.1 us
    unnamed x5, local copies, waits for them, and re-layouts  2.43 us

profile of v9, /device:TPU:97, one launch (start us, length us, event | category | flops | bytes accessed | tf_op | source)
XLA Modules:
  0.0 56.6 jit_solution(12708271973057826050)
XLA Ops:
  1.3 0.0 copy-start
  1.3 0.9 %copy-done = bf16[1024,128]{1,0:T(8,128)(2,1)S(1)} copy-done((bf16[1024,128]{1,0:T(8,128)(2,1)S(1)}, bf16[1024,128]{1,0:T(8,128)(2,1)}, u32[]{:S(2)}) %copy-start) | copy-done | bytes 262168
  2.2 0.0 copy-start.1
  2.2 0.7 %copy-done.1 = f32[1024]{0:T(1024)S(1)} copy-done((f32[1024]{0:T(1024)S(1)}, f32[1024]{0:T(1024)}, u32[]{:S(2)}) %copy-start.1) | copy-done | bytes 4120
  2.9 51.1 %pair_forces.1 = (f32[1024,128]{1,0:T(8,128)S(1)}, f32[1]{0:T(128)}) custom-call(bf16[1024,128]{1,0:T(8,128)(2,1)S(1)} %copy-done, f32[8,128]{1,0:T(8,128)S(1)} %bitcast.1, s32[1]{0:T(128)S(6)} %copy.7.cnt_ref), custom_call_target="tpu_custom_call" | custom-call | tf_op jit(solution)/shard_map/pair_forces/pallas_call | solution.py:299
  54.0 0.8 %copy.8 = f32[1024,128]{1,0:T(8,128)} copy(f32[1024,128]{1,0:T(8,128)S(1)} %get-tuple-element.4) | data formatting | bytes 1048576
Async XLA Ops:
  1.3 1.0 %copy-start = (bf16[1024,128]{1,0:T(8,128)(2,1)S(1)}, bf16[1024,128]{1,0:T(8,128)(2,1)}, u32[]{:S(2)}) copy-start(bf16[1024,128]{1,0:T(8,128)(2,1)} %x_ref.1) | copy-start | bytes 786436
  2.2 0.7 %copy-start.1 = (f32[1024]{0:T(1024)S(1)}, f32[1024]{0:T(1024)}, u32[]{:S(2)}) copy-start(f32[1024]{0:T(1024)} %param.4) | copy-start | bytes 12292
